TPU v7x, 256 devices: a whole 4x4x8 slice. The times are simulated.
256 devices in a mesh: pipe: 4 (over x), seq: 64 (over z, y, core).
Axes of the slice: x: 4, y: 4, z: 8, core: 2. Of those that a mesh axis runs over, the one named last changes fastest.
Arguments:
- previous: bfloat16 [4, 8192, 8192], P('pipe', 'seq'), may hold values from -6 to 6
- saved_head_inputs: bfloat16 [4, 8192, 8192], P('pipe', 'seq'), may hold values from -0.29882812 to 0.29882812
- input_b: bfloat16 [4, 8192, 1024], P('pipe', 'seq'), may hold values from -0.5 to 0.5
- input_c: bfloat16 [4, 8192, 1024], P('pipe', 'seq'), may hold values from -0.5 to 0.5
- steps: float32 [4, 8192, 128], P('pipe', 'seq'), may hold values from 0.1 to 13107.2, as said below
- decay_rate: float32 [4, 128], P('pipe'), may hold values from 3.0517578e-05 to 0.05
- skip_gain: float32 [4, 128], P('pipe'), may hold values from 0.5 to 1.5
- segment_ids: int32 [4, 8192], P('pipe', 'seq'), may hold values from 0 to 7, never falling along the last dimension, each value on 1 to 4096 neighbouring positions
- advantage_mask: int32 [8192], P('seq'), may hold values 0 or 1
Outputs:
- grad_x: bfloat16 [4, 8192, 8192], P('pipe', 'seq')
- grad_b: bfloat16 [4, 8192, 1024], P('pipe', 'seq')
- grad_c: bfloat16 [4, 8192, 1024], P('pipe', 'seq')
- bypass_gain_adjoint: float32 [4, 128], P('pipe')
Inputs may be any that keep to these rules, and one draw needn't show every extreme that they name: `steps`: Positive; in a few positions of each section the step is 1.6 * 8192 for every head.
All inputs are finite; a program needn't handle non-finite values. No bound on the sum of `advantage_mask` on one device may be relied on, other than what follows from the above.
Results may differ from a plain program's by a relative error of at most 0.0095.
Values may be sent and summed in bfloat16 or wider, within the bound.
A program may use at most 128 MiB of HBM per device.

v0:
```python
import jax
import jax.numpy as jnp
from jax import lax
from jax.sharding import Mesh
from jax.sharding import PartitionSpec as P

STATE = 128
BLOCK = 256
SEQ = ("seq_0", "seq_1", "seq_2")


def from_behind(value, axis, steps):
    count = lax.axis_size(axis)
    initial, last = (max(0, -steps), min(count, count - steps))
    return lax.ppermute(value, axis, [(source, source + steps) for source in range(initial, last)])


def one_axis_at_a_time(shard, axes):
    for axis in axes:
        shard = lax.psum(shard, axis)
    return shard


def in_order(parts, dim):
    parts = jnp.moveaxis(parts, 0, dim)
    lengths = parts.shape
    return parts.reshape(*lengths[:dim], lengths[dim] * lengths[dim + 1], *lengths[dim + 2 :])


def copy_for_each(shard, axis):
    copies = jnp.broadcast_to(shard, (lax.axis_size(axis), *shard.shape))
    return lax.all_to_all(copies, axis, split_axis=0, concat_axis=0, tiled=True)


def gathered_copies(shard, axis, dim):
    return in_order(copy_for_each(shard, axis), dim)


def swapped(block, axis, distance):
    count = lax.axis_size(axis)
    route = []
    for low in range(count):
        high = low | 1 << distance
        if high != low and high < count:
            route += [(low, high), (high, low)]
    return lax.ppermute(block, axis, route)


def mix(form, left, right):
    return jnp.einsum(form, left, right, preferred_element_type=jnp.float32)


def block_factors(seg, prev, steps_here, rate):
    cum = jnp.cumsum(-steps_here * rate[None, :], axis=0)
    enter = jnp.exp(cum) * (seg == prev)[:, None].astype(jnp.float32)
    leave = jnp.exp(cum[-1][None, :] - cum) * (seg == seg[-1])[:, None].astype(jnp.float32)
    through = jnp.exp(cum[-1]) * (seg[-1] == prev).astype(jnp.float32)
    return (cum, enter, leave, through)


def block_kernel(seg, cum):
    length = seg.shape[0]
    row = lax.broadcasted_iota(jnp.int32, (length, length), 0)
    col = lax.broadcasted_iota(jnp.int32, (length, length), 1)
    link = (seg[:, None] == seg[None, :]) & (row >= col)
    heads_first = jnp.transpose(cum)
    spread = heads_first[:, :, None] - heads_first[:, None, :]
    return jnp.exp(jnp.where(link[None, :, :], spread, -1e30))


def piece_backward(
    grad, inputs, bmat, cmat, steps_here, seg_here, first_prev, rate, skip, carry_fn
):
    tokens = grad.shape[0]
    heads = rate.shape[0]
    head_dim = grad.shape[1] // heads
    blocks = tokens // BLOCK
    grads = grad.reshape(blocks, BLOCK, heads, head_dim)
    inputs4 = inputs.reshape(blocks, BLOCK, heads, head_dim)
    bmats = bmat.reshape(blocks, BLOCK, STATE)
    cmats = cmat.reshape(blocks, BLOCK, STATE)
    segs = seg_here.reshape(blocks, BLOCK)
    prevs = jnp.concatenate([jnp.reshape(first_prev, (1,)), segs[:-1, -1]])
    step_blocks = steps_here.reshape(blocks, BLOCK, heads)
    items = (segs, prevs, step_blocks, grads, inputs4, bmats, cmats)

    def first_pass(item):
        seg, prev, steps_block, grad3, inputs3, bmat2, cmat2 = item
        cum, enter, leave, through = block_factors(seg, prev, steps_block, rate)
        xo = (leave[:, :, None] * inputs3).astype(jnp.bfloat16)
        gi = (enter[:, :, None] * grad3).astype(jnp.bfloat16)
        state = mix("tkp,tn->kpn", xo, bmat2)
        adjoint = mix("tkp,tn->kpn", gi, cmat2)
        return (through, state, adjoint, xo, gi)

    through, states, adjoints, xos, gis = lax.map(first_pass, items)
    zeros = jnp.zeros((heads, head_dim, STATE), jnp.float32)
    ones = jnp.ones((heads,), jnp.float32)

    def forward(carry, item):
        total, factor = carry
        return ((total * item[0][:, None, None] + item[1], factor * item[0]), (total, factor))

    def backward(carry, item):
        total, factor = carry
        return ((item[1] + item[0][:, None, None] * total, factor * item[0]), (total, factor))

    (fwd_total, fwd_factor), (local_in, factor_in) = lax.scan(
        forward, (zeros, ones), (through, states)
    )
    (bwd_total, discarded_result), (local_out, exiting_multiplier) = lax.scan(
        backward, (zeros, ones), (through, adjoints), reverse=True
    )
    earlier, after = carry_fn(fwd_total, fwd_factor, bwd_total)
    entering_state = (local_in + factor_in[:, :, None, None] * earlier[None]).astype(jnp.bfloat16)
    later = (local_out + exiting_multiplier[:, :, None, None] * after[None]).astype(jnp.bfloat16)

    def second_pass(item):
        seg, prev, steps_block, grad3, inputs3, bmat2, cmat2, xo, gi, enter_state, later_state = (
            item
        )
        cum, enter, leave, unused_through = block_factors(seg, prev, steps_block, rate)
        kernel = block_kernel(seg, cum)
        prod = mix("tkp,ukp->ktu", grad3, inputs3)
        w_one = (prod * kernel).astype(jnp.bfloat16)
        cross = mix("tn,un->tu", bmat2, cmat2)
        w_two = (jnp.swapaxes(kernel, 1, 2) * cross[None, :, :]).astype(jnp.bfloat16)
        grad_c = mix("ktu,un->tn", w_one, bmat2) + mix("tkp,kpn->tn", gi, enter_state)
        grad_b = mix("kut,un->tn", w_one, cmat2) + mix("tkp,kpn->tn", xo, later_state)
        grad_x = mix("ktu,ukp->tkp", w_two, grad3) + leave[:, :, None] * mix(
            "tn,kpn->tkp", bmat2, later_state
        )
        grad_x = grad_x + skip[None, :, None] * grad3.astype(jnp.float32)
        return (grad_x, grad_b, grad_c)

    grad_x, grad_b, grad_c = lax.map(second_pass, items + (xos, gis, entering_state, later))
    return (
        grad_x.reshape(tokens, heads * head_dim),
        grad_b.reshape(tokens, STATE),
        grad_c.reshape(tokens, STATE),
    )


def butterfly(buffer, send):
    slots = buffer.shape[0]
    place = lax.axis_index(SEQ)
    level = 0
    while 1 << level < slots:
        mine = place >> level & 1
        view = buffer.reshape((slots >> level + 1, 2, 1 << level) + buffer.shape[1:])
        half = lax.dynamic_index_in_dim(view, 1 - mine, 1, keepdims=False)
        received = send(half, level)
        view = lax.dynamic_update_index_in_dim(view, jnp.expand_dims(received, 1), 1 - mine, 1)
        buffer = view.reshape(buffer.shape)
        level += 1
    return buffer


def sweep(value, decays, piece, direction, pieces, send):
    value = send(value, direction)
    reach = 1
    while reach < pieces - 1:
        factor = jnp.ones((decays.shape[1],), jnp.float32)
        for offset in range(reach):
            index = piece - direction * (1 + offset)
            inside = (index >= 0) & (index < pieces)
            picked = lax.dynamic_index_in_dim(
                decays, jnp.clip(index, 0, pieces - 1), 0, keepdims=False
            )
            factor = factor * jnp.where(inside, picked, 1.0)
        value = value + factor[:, None, None] * send(value, direction * reach)
        reach = reach * 2
    return value


def on_device(
    previous,
    saved_head_inputs,
    input_b,
    input_c,
    steps,
    decay_rate,
    skip_gain,
    segment_ids,
    advantage_mask,
):
    section = lax.axis_index("pipe")
    arrived = from_behind(previous, "pipe", -1)
    masked = previous * advantage_mask.astype(jnp.bfloat16)[None, :, None]
    incoming = jnp.where(section == lax.axis_size("pipe") - 1, masked, arrived)[0]
    length = incoming.shape[0]
    heads = decay_rate.shape[1]
    head_dim = incoming.shape[1] // heads
    groups = input_b.shape[2] // STATE
    members = heads // groups
    devices = lax.axis_size(SEQ)
    place = lax.axis_index(SEQ)
    grad3 = incoming.reshape(length, heads, head_dim)
    inputs3 = saved_head_inputs[0].reshape(length, heads, head_dim)
    skip_part = mix("thp,thp->h", grad3, inputs3)
    bypass_gain_adjoint = one_axis_at_a_time(skip_part, SEQ)
    seg_all = gathered_copies(segment_ids[0], SEQ, 0)
    width = members * head_dim
    bundle = jnp.concatenate(
        [
            incoming.reshape(length, groups, width),
            saved_head_inputs[0].reshape(length, groups, width),
            input_b[0].reshape(length, groups, STATE),
            input_c[0].reshape(length, groups, STATE),
        ],
        axis=2,
    )
    bundle = jnp.swapaxes(bundle, 0, 1)

    def send_pieces(half, level):
        return swapped(half, SEQ, level)

    def send_steps(half, level):
        return swapped(half.astype(jnp.bfloat16), SEQ, level).astype(half.dtype)

    def send_results(half, level):
        return swapped(half, SEQ, level)

    gathered_values = butterfly(bundle, send_pieces).reshape(groups * length, 2 * width + 2 * STATE)
    grad_piece = gathered_values[:, :width]
    inputs_piece = gathered_values[:, width : 2 * width]
    b_piece = gathered_values[:, 2 * width : 2 * width + STATE]
    c_piece = gathered_values[:, 2 * width + STATE :]
    step_slots = jnp.swapaxes(steps[0].reshape(length, groups, members), 0, 1)
    steps_piece = butterfly(step_slots, send_steps).reshape(groups * length, members)
    group = place % groups
    piece = place // groups
    span = groups * length
    pieces = devices // groups
    seg_piece = lax.dynamic_slice_in_dim(seg_all, piece * span, span)
    before = lax.dynamic_index_in_dim(seg_all, jnp.maximum(piece * span - 1, 0), 0, keepdims=False)
    first_prev = jnp.where(piece > 0, before, -1)
    rate = lax.dynamic_slice_in_dim(decay_rate[0], group * members, members)
    skip = lax.dynamic_slice_in_dim(skip_gain[0], group * members, members)

    def send_state(value, distance):
        return from_behind(value.astype(jnp.bfloat16), SEQ, distance * groups).astype(value.dtype)

    def carry_across(total, factor, adjoint_total):
        table = gathered_copies(factor, SEQ, 0).reshape(pieces, groups, members)
        decays = lax.dynamic_index_in_dim(table, group, 1, keepdims=False)
        earlier = sweep(total, decays, piece, 1, pieces, send_state)
        after = sweep(adjoint_total, decays, piece, -1, pieces, send_state)
        return (earlier, after)

    grad_x_p, grad_b_p, grad_c_p = piece_backward(
        grad_piece,
        inputs_piece,
        b_piece,
        c_piece,
        steps_piece,
        seg_piece,
        first_prev,
        rate,
        skip,
        carry_across,
    )
    results = jnp.concatenate(
        [
            grad_x_p.astype(jnp.bfloat16),
            grad_b_p.astype(jnp.bfloat16),
            grad_c_p.astype(jnp.bfloat16),
        ],
        axis=1,
    )
    results = results.reshape(groups, length, width + 2 * STATE)
    returned = jnp.swapaxes(butterfly(results, send_results), 0, 1)
    grad_x_out = returned[:, :, :width].reshape(1, length, heads * head_dim)
    grad_b_out = returned[:, :, width : width + STATE].reshape(1, length, groups * STATE)
    grad_c_out = returned[:, :, width + STATE :].reshape(1, length, groups * STATE)
    return (grad_x_out, grad_b_out, grad_c_out, bypass_gain_adjoint.reshape(1, heads))


def solution(mesh):
    finer = Mesh(
        mesh.devices.reshape(mesh.shape["pipe"], 8, 4, 2), ("pipe", "seq_0", "seq_1", "seq_2")
    )
    return jax.shard_map(
        on_device,
        mesh=finer,
        in_specs=(
            P("pipe", SEQ, None),
            P("pipe", SEQ, None),
            P("pipe", SEQ, None),
            P("pipe", SEQ, None),
            P("pipe", SEQ, None),
            P("pipe", None),
            P("pipe", None),
            P("pipe", SEQ),
            P(SEQ),
        ),
        out_specs=(
            P("pipe", SEQ, None),
            P("pipe", SEQ, None),
            P("pipe", SEQ, None),
            P("pipe", None),
        ),
        check_vma=False,
    )
```

profile of v0, /device:TPU:1, one launch (start us, length us, event | category | flops | bytes accessed | tf_op | source)
XLA Modules:
  0.0 627.6 jit_solution(1278346177308721672)
XLA Ops:
  0.7 4.1 copy.128
  6.1 3.3 copy.130
  9.7 42.3 %collective-permute-done = bf16[1,128,8192]{1,2,0:T(8,128)(2,1)} collective-permute-done((bf16[1,128,8192]{1,2,0:T(8,128)(2,1)}, bf16[1,128,8192]{1,2,0:T(8,128)(2,1)}, u32[]{:S(2)}, u32[]{:S(2)}) %collective-permute-start) | collective-permute-done | bytes 2097184 | tf_op jit(solution)/shard_map/ppermute | solution.py:15
  52.1 2.4 multiply_select_fusion
  56.0 2.3 maximum_bitcast_fusion
  58.3 6.8 %copy.133 = bf16[8,128,2304]{2,1,0:T(8,128)(2,1)} copy(bf16[8,128,2304]{1,2,0:T(8,128)(2,1)} %maximum_bitcast_fusion) | data formatting | bytes 9437184 | tf_op jit(solution)/shard_map/transpose | solution.py:213
  65.1 3.3 dynamic-slice_bitcast_fusion.2
  68.3 3.5 collective-permute-start.1
  71.8 4.4 collective-permute-done.1
  77.7 3.3 dynamic-slice_bitcast_fusion.1
  82.5 51.2 %collective-permute-done.2 = bf16[2,2,128,2304]{3,2,1,0:T(8,128)(2,1)S(1)} collective-permute-done((bf16[2,2,128,2304]{3,2,1,0:T(8,128)(2,1)}, bf16[2,2,128,2304]{3,2,1,0:T(8,128)(2,1)S(1)}, u32[]{:S(2)}, u32[]{:S(2)}) %collective-permute-start.2) | collective-permute-done | bytes 2359328 | tf_op jit(solution)/shard_map/ppermute | solution.py:46
  135.4 3.3 dynamic-slice_bitcast_fusion
  138.7 3.0 collective-permute-start.3
  145.4 10.9 %all-to-all-start = ((s32[64,1,128]{2,1,0:T(1,128)}), s32[64,1,128]{2,1,0:T(1,128)S(1)}, u32[]{:S(2)}, u32[]{:S(2)}) async-start(s32[64,1,128]{2,1,0:T(1,128)} %broadcast_in_dim.156), calls=%async_computation | async-start | bytes 65536 | tf_op jit(solution)/shard_map/all_to_all | solution.py:32
  156.4 36.8 %collective-permute-done.5 = bf16[2,2,128,16]{2,1,3,0:T(2,128)(2,1)S(1)} collective-permute-done((bf16[2,2,128,16]{2,1,3,0:T(2,128)(2,1)S(1)}, bf16[2,2,128,16]{2,1,3,0:T(2,128)(2,1)S(1)}, u32[]{:S(2)}, u32[]{:S(2)}) %collective-permute-start.5) | collective-permute-done | bytes 16416 | tf_op jit(solution)/shard_map/ppermute | solution.py:46
  195.2 2.4 collective-permute-done.6
  199.3 3.2 bitcast_dynamic-update-slice_fusion.3
  202.5 4.0 fusion.103
  208.3 6.4 %reshape.402 = bf16[4,256,16,64]{3,2,1,0:T(8,128)(2,1)} reshape(bf16[1024,1024]{1,0:T(8,128)(2,1)} %get-tuple-element.698) | data formatting | bytes 4194304 | tf_op jit(solution)/shard_map/reshape | solution.py:79
  214.6 5.8 copy.144
  220.5 4.0 reshape.400
  224.4 4.8 copy.148
  232.5 45.0 %while.70 = (s32[]{:T(128)}, f32[4,16]{1,0:T(4,128)S(1)}, f32[4,16,64,128]{3,2,1,0:T(8,128)}, f32[4,16,64,128]{3,2,1,0:T(8,128)}, bf16[4,256,16,64]{1,3,2,0:T(8,...) while((s32[]{:T(128)}, f32[4,16]{1,0:T(4,128)S(1)}, ...), condition=%wide.region_3.4_spmd, body=%wide.region_0.3_spmd.sunk | while | flops 137913408 | bytes 4549431 | solution.py:96
  237.2 2.3 fusion.150
  241.4 2.1 fusion.148
  248.5 2.3 fusion.150
  252.7 2.1 fusion.148
  259.7 2.3 fusion.150
  264.0 2.1 fusion.148
  271.0 2.3 fusion.150
  275.2 2.1 fusion.148
  279.1 8.2 %while.73 = (s32[]{:T(128)}, f32[16,64,128]{2,1,0:T(8,128)S(1)}, f32[16]{0:T(128)S(1)}, f32[4,16,64,128]{3,2,1,0:T(8,128)}, f32[4,16]{1,0:T(4,128)S(1)}, /*index...) while((s32[]{:T(128)}, f32[16,64,128]{2,1,0:T(8,128)S(1)}, ...), condition=%wide.region_5.6_spmd.clone, body=%wide.region_4.5_spmd.clone.sunk | while | flops 524323 | bytes 2622581 | solution.py:108
  288.1 3.5 collective-permute-start.11
  293.2 8.3 %while.72 = (s32[]{:T(128)}, f32[16,64,128]{2,1,0:T(8,128)S(1)}, f32[16]{0:T(128)S(1)}, f32[4,16,64,128]{3,2,1,0:T(8,128)}, f32[4,16]{1,0:T(4,128)S(1)}, /*index...) while((s32[]{:T(128)}, f32[16,64,128]{2,1,0:T(8,128)S(1)}, ...), condition=%wide.region_7.8_spmd.clone, body=%wide.region_6.7_spmd.clone.sunk | while | flops 524324 | bytes 2622093 | solution.py:111
  303.6 4.2 collective-permute-start.12
  308.4 14.0 %all-to-all-start.1 = ((f32[64,1,16]{2,1,0:T(1,128)}), f32[64,1,16]{2,1,0:T(1,128)S(1)}, u32[]{:S(2)}, u32[]{:S(2)}) async-start(f32[64,1,16]{2,1,0:T(1,128)} %broadcast_in_dim.164), calls=%async_computation.1 | async-start | bytes 65536 | tf_op jit(solution)/shard_map/all_to_all | solution.py:32
  322.5 9.2 %all-to-all-done.1 = f32[64,1,16]{2,1,0:T(1,128)S(1)} async-done(((f32[64,1,16]{2,1,0:T(1,128)}), f32[64,1,16]{2,1,0:T(1,128)S(1)}, u32[]{:S(2)}, u32[]{:S(2)}) %all-to-all-start.1) | async-done | bytes 4128 | tf_op jit(solution)/shard_map/all_to_all | solution.py:32
  333.2 4.1 collective-permute-start.13
  337.3 3.5 collective-permute-done.8
  344.6 8.4 %collective-permute-start.14 = (bf16[16,64,128]{2,1,0:T(8,128)(2,1)}, bf16[16,64,128]{2,1,0:T(8,128)(2,1)}, u32[]{:S(2)}, u32[]{:S(2)}) collective-permute-start(bf16[16,64,128]{2,1,0:T(8,128)(2,1)} %fusion.78), channel_id=1, source_target_pairs={{0,32},{1,33},{2,34},{3,35},{4,36},{5,37},{6,38},{7,39},{8,40},{9,... | collective-permute-start | bytes 786440 | tf_op jit(solution)/shard_map/ppermute | solution.py:15
  353.1 4.6 collective-permute-done.9
  363.2 11.0 %collective-permute-done.10 = bf16[16,64,128]{2,1,0:T(8,128)(2,1)S(1)} collective-permute-done((bf16[16,64,128]{2,1,0:T(8,128)(2,1)S(1)}, bf16[16,64,128]{2,1,0:T(8,128)(2,1)S(1)}, u32[]{:S(2)}, u32[]{:S(2)}) %collective-permute-start.10) | collective-permute-done | bytes 262176 | tf_op jit(solution)/shard_map/ppermute | solution.py:15
  376.8 57.8 %while.71 = (s32[]{:T(128)}, bf16[4,256,16,64]{1,3,2,0:T(8,128)(2,1)}, bf16[4,256,128]{2,1,0:T(8,128)(2,1)}, bf16[4,256,128]{2,1,0:T(8,128)(2,1)}, bf16[4,256,16...) while((s32[]{:T(128)}, ...), condition=%wide.region_12.13_spmd, body=%wide.region_8.12_spmd.sunk | while | flops 532828736 | bytes 14336141 | solution.py:136
  381.4 2.1 fusion.171
  383.5 2.6 convert_reduce_fusion.2
  398.0 2.6 convert_reduce_fusion.2
  412.4 2.6 convert_reduce_fusion.2
  426.9 2.6 convert_reduce_fusion.2
  434.6 4.0 convert_element_type.223
  439.1 16.9 %pad_maximum_fusion = bf16[4,2,1,128,1280]{3,1,4,0,2:T(2,128)(2,1)S(1)} fusion(bf16[4,2,1,128,128]{3,1,4,0,2:T(2,128)(2,1)S(1)} %copy.152, bf16[4,2,1,128,128]{3,1,4,0,2:T(2,128)(2,1)S(1)} %copy.151, bf16[4,2,1,128,1024]{3,1,4,0,2:T(2,128)(2,1)} %convert_element_type.223), kind=kLoop, calls=%fused_computation.120 | loop fusion | flops 2621440 | bytes 5242880 | tf_op jit(solution)/shard_map/concatenate | solution.py:263
  455.9 4.1 constant_dynamic-slice_fusion.5
  460.0 6.1 copy.153
  466.9 3.0 collective-permute-done.15
  469.9 6.3 %copy.154 = bf16[4,1,1,128,1280]{3,1,4,0,2:T(2,128)(2,1)} copy(bf16[4,1,1,128,1280]{4,3,0,2,1:T(8,128)(2,1)} %bitcast.86) | data formatting | bytes 2621440 | tf_op jit(solution)/shard_map/broadcast_in_dim | solution.py:153
  476.2 65.0 %dynamic_update_slice.95 = bf16[4,2,1,128,1280]{3,1,4,0,2:T(2,128)(2,1)S(1)} dynamic-update-slice(bf16[4,2,1,128,1280]{3,1,4,0,2:T(2,128)(2,1)S(1)} %pad_maximum_fusion, bf16[4,1,1,128,1280]{3,1,4,0,2:T(2,128)(2,1)} %copy.154, s32[]{:T(128)} %constant.416.clone.1, s32[]{:T(128)S(6)} %select_n.240, s32[]{:T(128)} %constant.416.clone.1, s32[]{:T(128)} %constant.416.clone.1, s32[]{:T(128)} %constant.416.clone.1) | dynamic-update-slice | bytes 2621444 | tf_op jit(solution)/shard_map/jit(dynamic_update_index_in_dim)/dynamic_update_slice | solution.py:153
  543.0 4.2 copy.155
  547.6 4.7 copy.156
  552.3 25.3 %collective-permute-done.16 = bf16[2,2,128,1280]{3,2,1,0:T(8,128)(2,1)} collective-permute-done((bf16[2,2,128,1280]{3,2,1,0:T(8,128)(2,1)}, bf16[2,2,128,1280]{3,2,1,0:T(8,128)(2,1)}, u32[]{:S(2)}, u32[]{:S(2)}) %collective-permute-start.16) | collective-permute-done | bytes 1310752 | tf_op jit(solution)/shard_map/ppermute | solution.py:46
  577.5 2.5 bitcast_dynamic-update-slice_fusion.6
  580.0 2.5 dynamic-slice_bitcast_fusion.3
  584.5 14.0 %psum.21 = f32[128]{0:T(128)S(1)} all-reduce(f32[128]{0:T(128)S(1)} %fusion.74), channel_id=1, replica_groups=mesh['pipe'=4,'seq_0'=8,'seq_1'=4,'seq_2'=2] {'seq_0'}, use_global_device_ids=true, to_apply=%region_13.14 | all-reduce | flops 128 | bytes 1024 | tf_op jit(solution)/shard_map/psum | solution.py:20
  598.5 16.7 %psum.22 = f32[128]{0:T(128)S(1)} all-reduce(f32[128]{0:T(128)S(1)} %psum.21), channel_id=1, replica_groups=mesh['pipe'=4,'seq_0'=8,'seq_1'=4,'seq_2'=2] {'seq_1'}, use_global_device_ids=true, to_apply=%region_14.15 | all-reduce | flops 128 | bytes 1024 | tf_op jit(solution)/shard_map/psum | solution.py:20
  615.2 5.1 psum.23
  623.3 2.3 reshape.379
  (334 shorter events, 133.0 us)
Async XLA Ops:
  0.6 194.5 %copy-start = (f32[1,128]{1,0:T(1,128)S(1)}, f32[1,128]{1,0:T(1,128)}, u32[]{:S(2)}) copy-start(f32[1,128]{1,0:T(1,128)} %param.22) | copy-start | bytes 1540
  0.6 5.4 copy-start.22
  4.7 47.3 %collective-permute-start = (bf16[1,128,8192]{1,2,0:T(8,128)(2,1)}, bf16[1,128,8192]{1,2,0:T(8,128)(2,1)}, u32[]{:S(2)}, u32[]{:S(2)}) collective-permute-start(bf16[1,128,8192]{1,2,0:T(8,128)(2,1)} %copy.128), channel_id=1, source_target_pairs={{64,0},{128,64},{192,128},{65,1},{129,65},{193,129},{66,2},{130,66... | collective-permute-start | bytes 6291464 | tf_op jit(solution)/shard_map/ppermute | solution.py:15
  6.1 3.3 copy-start.12
  6.1 3.5 copy-start.13
  9.4 45.1 %copy-start.2 = (bf16[1,128,8192]{1,2,0:T(8,128)(2,1)}, bf16[1,128,8192]{1,2,0:T(8,128)(2,1)S(1)}, u32[]{:S(2)}) copy-start(bf16[1,128,8192]{1,2,0:T(8,128)(2,1)S(1)} %copy.130) | copy-start | bytes 6291460
  54.5 1.4 copy-start.4
  68.3 7.9 %collective-permute-start.1 = (bf16[4,1,128,2304]{3,2,0,1:T(8,128)(2,1)}, bf16[4,1,128,2304]{3,2,0,1:T(8,128)(2,1)S(1)}, u32[]{:S(2)}, u32[]{:S(2)}) collective-permute-start(bf16[4,1,128,2304]{3,2,0,1:T(8,128)(2,1)} %dynamic-slice_bitcast_fusion.2), channel_id=1, source_target_pairs={{0,1},{1,0},{2,3},{3,2},{4,5},{5,4},{6,7},{7,6},{8,9},{9,8},{10,11... | collective-permute-start | bytes 7077896 | tf_op jit(solution)/shard_map/ppermute | solution.py:46
  81.0 52.8 %collective-permute-start.2 = (bf16[2,2,128,2304]{3,2,1,0:T(8,128)(2,1)}, bf16[2,2,128,2304]{3,2,1,0:T(8,128)(2,1)S(1)}, u32[]{:S(2)}, u32[]{:S(2)}) collective-permute-start(bf16[2,2,128,2304]{3,2,1,0:T(8,128)(2,1)} %dynamic-slice_bitcast_fusion.1), channel_id=1, source_target_pairs={{0,2},{2,0},{1,3},{3,1},{4,6},{6,4},{5,7},{7,5},{8,10},{10,8},{9,1... | collective-permute-start | bytes 7077896 | tf_op jit(solution)/shard_map/ppermute | solution.py:46
  135.4 6.3 %copy-start.20 = (f32[1,128,128]{2,1,0:T(8,128)S(1)}, f32[1,128,128]{2,1,0:T(8,128)}, u32[]{:S(2)}) copy-start(f32[1,128,128]{2,1,0:T(8,128)} %param.21) | copy-start | bytes 196612
  135.4 9.4 %copy-start.21 = (s32[1,128]{1,0:T(1,128)S(1)}, s32[1,128]{1,0:T(1,128)}, u32[]{:S(2)}) copy-start(s32[1,128]{1,0:T(1,128)} %param.24) | copy-start | bytes 1540
  138.7 60.5 %collective-permute-start.3 = (bf16[1,4,128,2304]{3,2,1,0:T(8,128)(2,1)}, bf16[1,4,128,2304]{3,2,1,0:T(8,128)(2,1)}, u32[]{:S(2)}, u32[]{:S(2)}) collective-permute-start(bf16[1,4,128,2304]{3,2,1,0:T(8,128)(2,1)} %dynamic-slice_bitcast_fusion), channel_id=1, source_target_pairs={{0,4},{4,0},{1,5},{5,1},{2,6},{6,2},{3,7},{7,3},{8,12},{12,8},{9,1... | collective-permute-start | bytes 7077896 | tf_op jit(solution)/shard_map/ppermute | solution.py:46
  141.9 2.4 collective-permute-start.4
  144.3 48.9 %collective-permute-start.5 = (bf16[2,2,128,16]{2,1,3,0:T(2,128)(2,1)S(1)}, bf16[2,2,128,16]{2,1,3,0:T(2,128)(2,1)S(1)}, u32[]{:S(2)}, u32[]{:S(2)}) collective-permute-start(bf16[2,2,128,16]{2,1,3,0:T(2,128)(2,1)S(1)} %bitcast.432), channel_id=1, source_target_pairs={{0,2},{2,0},{1,3},{3,1},{4,6},{6,4},{5,7},{7,5},{8,10},{10,8},{9,1... | collective-permute-start | bytes 49160 | tf_op jit(solution)/shard_map/ppermute | solution.py:46
  145.4 52.3 %all-to-all-start = ((s32[64,1,128]{2,1,0:T(1,128)}), s32[64,1,128]{2,1,0:T(1,128)S(1)}, u32[]{:S(2)}, u32[]{:S(2)}) async-start(s32[64,1,128]{2,1,0:T(1,128)} %broadcast_in_dim.156), calls=%async_computation | async-start | bytes 65536 | tf_op jit(solution)/shard_map/all_to_all | solution.py:32
  193.3 4.4 collective-permute-start.6
  288.1 15.5 %collective-permute-start.11 = (bf16[16,64,128]{2,1,0:T(8,128)(2,1)}, bf16[16,64,128]{2,1,0:T(8,128)(2,1)S(1)}, u32[]{:S(2)}, u32[]{:S(2)}) collective-permute-start(bf16[16,64,128]{2,1,0:T(8,128)(2,1)} %convert_element_type.214), channel_id=1, source_target_pairs={{0,8},{1,9},{2,10},{3,11},{4,12},{5,13},{6,14},{7,15},{8,16},{9,17... | collective-permute-start | bytes 786440 | tf_op jit(solution)/shard_map/ppermute | solution.py:15
  301.5 51.5 %copy-start.23 = (f32[1,128]{1,0:T(1,128)S(1)}, f32[1,128]{1,0:T(1,128)}, u32[]{:S(2)}) copy-start(f32[1,128]{1,0:T(1,128)} %param.23) | copy-start | bytes 1540
  302.3 29.4 %collective-permute-start.7 = (bf16[16,64,128]{2,1,0:T(8,128)(2,1)}, bf16[16,64,128]{2,1,0:T(8,128)(2,1)S(1)}, u32[]{:S(2)}, u32[]{:S(2)}) collective-permute-start(bf16[16,64,128]{2,1,0:T(8,128)(2,1)} %convert_element_type.206), channel_id=1, source_target_pairs={{8,0},{9,1},{10,2},{11,3},{12,4},{13,5},{14,6},{15,7},{16,8},{17,9... | collective-permute-start | bytes 786440 | tf_op jit(solution)/shard_map/ppermute | solution.py:15
  303.6 29.5 %collective-permute-start.12 = (bf16[16,64,128]{2,1,0:T(8,128)(2,1)S(1)}, bf16[16,64,128]{2,1,0:T(8,128)(2,1)S(1)}, u32[]{:S(2)}, u32[]{:S(2)}) collective-permute-start(bf16[16,64,128]{2,1,0:T(8,128)(2,1)S(1)} %collective-permute-done.11), channel_id=1, source_target_pairs={{0,8},{1,9},{2,10},{3,11},{4,12},{5,13},{6,14},{7,15},{8,16},{9,17... | collective-permute-start | bytes 786440 | tf_op jit(solution)/shard_map/ppermute | solution.py:15
  308.4 23.3 %all-to-all-start.1 = ((f32[64,1,16]{2,1,0:T(1,128)}), f32[64,1,16]{2,1,0:T(1,128)S(1)}, u32[]{:S(2)}, u32[]{:S(2)}) async-start(f32[64,1,16]{2,1,0:T(1,128)} %broadcast_in_dim.164), calls=%async_computation.1 | async-start | bytes 65536 | tf_op jit(solution)/shard_map/all_to_all | solution.py:32
  331.7 9.1 %collective-permute-start.8 = (bf16[16,64,128]{2,1,0:T(8,128)(2,1)S(1)}, bf16[16,64,128]{2,1,0:T(8,128)(2,1)S(1)}, u32[]{:S(2)}, u32[]{:S(2)}) collective-permute-start(bf16[16,64,128]{2,1,0:T(8,128)(2,1)S(1)} %collective-permute-done.7), channel_id=1, source_target_pairs={{8,0},{9,1},{10,2},{11,3},{12,4},{13,5},{14,6},{15,7},{16,8},{17,9... | collective-permute-start | bytes 786440 | tf_op jit(solution)/shard_map/ppermute | solution.py:15
  333.2 9.8 %collective-permute-start.13 = (bf16[16,64,128]{2,1,0:T(8,128)(2,1)S(1)}, bf16[16,64,128]{2,1,0:T(8,128)(2,1)S(1)}, u32[]{:S(2)}, u32[]{:S(2)}) collective-permute-start(bf16[16,64,128]{2,1,0:T(8,128)(2,1)S(1)} %fusion.76), channel_id=1, source_target_pairs={{0,16},{1,17},{2,18},{3,19},{4,20},{5,21},{6,22},{7,23},{8,24},{9,... | collective-permute-start | bytes 786440 | tf_op jit(solution)/shard_map/ppermute | solution.py:15
  341.7 16.1 %collective-permute-start.9 = (bf16[16,64,128]{2,1,0:T(8,128)(2,1)}, bf16[16,64,128]{2,1,0:T(8,128)(2,1)}, u32[]{:S(2)}, u32[]{:S(2)}) collective-permute-start(bf16[16,64,128]{2,1,0:T(8,128)(2,1)} %fusion.75), channel_id=1, source_target_pairs={{16,0},{17,1},{18,2},{19,3},{20,4},{21,5},{22,6},{23,7},{24,8},{25... | collective-permute-start | bytes 786440 | tf_op jit(solution)/shard_map/ppermute | solution.py:15
  343.0 0.7 copy-start.9
  344.6 15.9 %collective-permute-start.14 = (bf16[16,64,128]{2,1,0:T(8,128)(2,1)}, bf16[16,64,128]{2,1,0:T(8,128)(2,1)}, u32[]{:S(2)}, u32[]{:S(2)}) collective-permute-start(bf16[16,64,128]{2,1,0:T(8,128)(2,1)} %fusion.78), channel_id=1, source_target_pairs={{0,32},{1,33},{2,34},{3,35},{4,36},{5,37},{6,38},{7,39},{8,40},{9,... | collective-permute-start | bytes 786440 | tf_op jit(solution)/shard_map/ppermute | solution.py:15
  353.1 8.7 %copy-start.7 = (f32[4,16,64,128]{3,2,1,0:T(8,128)S(1)}, f32[4,16,64,128]{3,2,1,0:T(8,128)}, u32[]{:S(2)}) copy-start(f32[4,16,64,128]{3,2,1,0:T(8,128)} %get-tuple-element.356) | copy-start | bytes 6291460
  359.0 15.2 %collective-permute-start.10 = (bf16[16,64,128]{2,1,0:T(8,128)(2,1)S(1)}, bf16[16,64,128]{2,1,0:T(8,128)(2,1)S(1)}, u32[]{:S(2)}, u32[]{:S(2)}) collective-permute-start(bf16[16,64,128]{2,1,0:T(8,128)(2,1)S(1)} %fusion.77), channel_id=1, source_target_pairs={{32,0},{33,1},{34,2},{35,3},{36,4},{37,5},{38,6},{39,7},{40,8},{41... | collective-permute-start | bytes 786440 | tf_op jit(solution)/shard_map/ppermute | solution.py:15
  361.9 13.6 %copy-start.8 = (f32[4,16,64,128]{3,2,1,0:T(8,128)S(1)}, f32[4,16,64,128]{3,2,1,0:T(8,128)}, u32[]{:S(2)}) copy-start(f32[4,16,64,128]{3,2,1,0:T(8,128)} %get-tuple-element.349) | copy-start | bytes 6291460
  376.8 2.0 copy-start.10
  383.5 4.2 copy-start.14
  386.2 4.2 copy-start.17
  386.2 5.1 copy-start.11
  388.8 1.8 copy-start.15
  390.6 0.7 copy-start.18
  391.3 2.0 copy-start.10
  398.0 4.2 copy-start.14
  400.6 4.2 copy-start.17
  400.6 5.1 copy-start.11
  403.2 1.8 copy-start.15
  405.0 0.7 copy-start.18
  405.7 2.0 copy-start.10
  412.4 4.2 copy-start.14
  415.1 4.2 copy-start.17
  415.1 5.1 copy-start.11
  417.7 1.8 copy-start.15
  419.5 0.7 copy-start.18
  420.2 2.0 copy-start.10
  426.9 4.2 copy-start.14
  429.5 4.2 copy-start.17
  429.6 5.1 copy-start.11
  432.2 1.8 copy-start.15
  433.9 0.7 copy-start.18
  434.6 4.0 copy-start.16
  434.6 4.2 copy-start.19
  466.1 3.8 collective-permute-start.15
  547.3 30.3 %collective-permute-start.16 = (bf16[2,2,128,1280]{3,2,1,0:T(8,128)(2,1)}, bf16[2,2,128,1280]{3,2,1,0:T(8,128)(2,1)}, u32[]{:S(2)}, u32[]{:S(2)}) collective-permute-start(bf16[2,2,128,1280]{3,2,1,0:T(8,128)(2,1)} %bitcast.413), channel_id=1, source_target_pairs={{0,2},{2,0},{1,3},{3,1},{4,6},{6,4},{5,7},{7,5},{8,10},{10,8},{9,1... | collective-permute-start | bytes 3932168 | tf_op jit(solution)/shard_map/ppermute | solution.py:46
  552.3 31.2 %copy-start.3 = (bf16[1,128,8192]{1,2,0:T(8,128)(2,1)S(1)}, bf16[1,128,8192]{1,2,0:T(8,128)(2,1)}, u32[]{:S(2)}) copy-start(bf16[1,128,8192]{1,2,0:T(8,128)(2,1)} %copy-done.2) | copy-start | bytes 6291460
  552.3 31.2 %copy-start.5 = (bf16[1,128,8192]{1,2,0:T(8,128)(2,1)S(1)}, bf16[1,128,8192]{1,2,0:T(8,128)(2,1)}, u32[]{:S(2)}) copy-start(bf16[1,128,8192]{1,2,0:T(8,128)(2,1)} %copy-done.4) | copy-start | bytes 6291460
  582.5 37.8 %collective-permute-start.17 = (bf16[1,4,128,1280]{3,2,1,0:T(8,128)(2,1)}, bf16[1,4,128,1280]{3,2,1,0:T(8,128)(2,1)}, u32[]{:S(2)}, u32[]{:S(2)}) collective-permute-start(bf16[1,4,128,1280]{3,2,1,0:T(8,128)(2,1)} %dynamic-slice_bitcast_fusion.3), channel_id=1, source_target_pairs={{0,4},{4,0},{1,5},{5,1},{2,6},{6,2},{3,7},{7,3},{8,12},{12,8},{9,1... | collective-permute-start | bytes 3932168 | tf_op jit(solution)/shard_map/ppermute | solution.py:46
  583.5 36.8 %copy-start.6 = (bf16[2,2,2,128,1280]{4,3,2,1,0:T(8,128)(2,1)S(1)}, bf16[2,2,2,128,1280]{4,3,2,1,0:T(8,128)(2,1)}, u32[]{:S(2)}) copy-start(bf16[2,2,2,128,1280]{4,3,2,1,0:T(8,128)(2,1)} %bitcast_dynamic-update-slice_fusion.6) | copy-start | bytes 7864324
  623.3 4.4 copy-start.1
where the time goes:
time: 635 us; the launch traced here: 628 us
  waiting for transfers between devices  195 us (31%)
  local copies, waits for them, and re-layouts  190 us (30%)
  other arithmetic  73 us (11%)
  starting transfers between devices  65.8 us (10%)
  matrix products  61 us (10%)
  blocking collectives  35.7 us (6%)
    ppermute x9, waiting for transfers between devices, swapped(): return lax.ppermute(block, axis, route)  124 us
    dynamic_update_slice x6, local copies, waits for them, and re-layouts, butterfly(): lax.dynamic_update_index_in_dim(view, jnp.expand_dims(received, 1), 1 - m...  75.3 us
    ppermute x9, waiting for transfers between devices, from_behind(): lax.ppermute(value, axis, [(source, source + steps) for source in range(i...  61.6 us
    dot_general x40, matrix products, mix(): return jnp.einsum(form, left, right, preferred_element_type=jnp.float32)  61 us
    psum x3, blocking collectives, one_axis_at_a_time(): shard = lax.psum(shard, axis)  35.7 us
    ppermute x9, starting transfers between devices, from_behind(): lax.ppermute(value, axis, [(source, source + steps) for source in range(i...  26.8 us
    all_to_all x2, starting transfers between devices, copy_for_each(): return lax.all_to_all(copies, axis, split_axis=0, concat_axis=0, tiled=True)  24.9 us
    concatenate x1, other arithmetic, on_device(): jnp.concatenate([grad_x_p.astype(jnp.bfloat16), grad_b_p.astype(jnp.bfloa...  16.9 us
  transfers between devices with their start and end apart: 20, of which 12 were waited for; matrix products, arithmetic and copies ran while one was open for 5% of the time, Pallas kernels for 0%

commit v1 on v0

v1 whole, which is shorter than its diff:
```python
import jax
import jax.numpy as jnp
from jax import lax
from jax.experimental import pallas as pl
from jax.experimental.pallas import tpu as pltpu
from jax.sharding import Mesh
from jax.sharding import PartitionSpec as P

SEQ = ("seq_0", "seq_1", "seq_2")
MESH = pl.DeviceIdType.MESH
F32 = jnp.float32
BF16 = jnp.bfloat16
NY = 4
T = 128
N = 128
H = 128
D = 64
GROUPS = 8
PAIRS = GROUPS // 2
QL = 256
QUARTERS = 32


def split(v, parts):
    out = []
    for _ in range(parts):
        piece = v.astype(BF16)
        out.append(piece)
        v = v - piece.astype(F32)
    return out


def dot(a, b):
    return lax.dot_general(a, b, (((1,), (0,)), ((), ())), preferred_element_type=F32)


def dot_nt(a, b):
    return lax.dot_general(a, b, (((1,), (1,)), ((), ())), preferred_element_type=F32)


def lanes_of(index, width):
    return pl.ds(pl.multiple_of(index * width, width), width)


def indicator(q, copies):
    row = lax.broadcasted_iota(jnp.int32, (H, QL), 0)
    col = lax.broadcasted_iota(jnp.int32, (H, QL), 1)
    one = jnp.where(row == 4 * q + lax.shift_right_logical(col, 6), 1.0, 0.0).astype(BF16)
    return jnp.concatenate([one] * copies, axis=0)


def make_kernel(nx, nz):
    def kernel(
        prev_ref, x_ref, b_ref, c_ref, steps_ref, rate_ref, skip_ref, seg_ref, mask_ref,
        gx_out, gb_out, gc_out, sk_out,
        grad, xo, gi, gxa, lexp, gca, gba, cum_s, cumt_s, bias_s, biast_s, lvs, ens, bt, ct,
        info_s, info_r, th_s, thx,
        st, sp, tt, tr, zs, zr, es, er, keep, epart, ex, tz_s,
        skp, sk_s, sk_r, skz_s, skz_r,
        gsend, grecv, isend, irecv, ssend, srecv, zsend, zrecv,
        dsend, drecv, tsend, trecv, csend, crecv, esend, erecv, psend, precv,
    ):
        px = lax.axis_index("pipe")
        z = lax.axis_index("seq_0")
        y = lax.axis_index("seq_1")
        c = lax.axis_index("seq_2")
        d = 2 * y + c

        def remote(src, dst, ssem, rsem, where):
            return pltpu.make_async_remote_copy(
                src_ref=src, dst_ref=dst, send_sem=ssem, recv_sem=rsem, device_id=where, device_id_type=MESH
            )

        def grad_copy(k):
            part = lanes_of(k, 2048)
            return remote(
                prev_ref.at[:, part], grad.at[:, part], gsend.at[k], grecv.at[k], (lax.rem(px + nx - 1, nx), z, y, c)
            )

        @pl.when(px > 0)
        def _():
            for k in range(PAIRS):
                grad_copy(k).start()

        row = lax.broadcasted_iota(jnp.int32, (T, T), 0)
        col = lax.broadcasted_iota(jnp.int32, (T, T), 1)
        cum = -(steps_ref[...] * rate_ref[...])
        for shift in (1, 2, 4, 8, 16, 32, 64):
            cum = cum + jnp.where(row >= shift, pltpu.roll(cum, shift, 0), 0.0)
        cum_s[...] = cum
        cumt_s[...] = cum.T
        last = cum[T - 1 : T, :]
        segrow = jnp.broadcast_to(seg_ref[...].astype(F32), (T, T))
        segcol = segrow.T
        seglast = segcol[T - 1 : T, :]
        info_s[0:1, :] = last
        info_s[1:2, :] = seglast
        info_s[2:8, :] = jnp.zeros((6, H), F32)
        info_r[d] = info_s[...]

        def plane_peer(off):
            other = lax.rem(d + off, 2 * NY)
            return (px, z, lax.div(other, 2), lax.rem(other, 2))

        def info_copy(off):
            return remote(info_s, info_r.at[d], isend.at[off - 1], irecv.at[off - 1], plane_peer(off))

        def info_next(other):
            return remote(
                info_s, info_r.at[2 * NY], isend.at[7 + other], irecv.at[7], (px, lax.rem(z + 1, nz), other // 2, other % 2)
            )

        for off in range(1, 2 * NY):
            info_copy(off).start()

        @pl.when((d == 2 * NY - 1) & (z < nz - 1))
        def _():
            for other in range(2 * NY):
                info_next(other).start()

        @pl.when(z == 0)
        def _():
            info_r[2 * NY] = jnp.full((8, H), -1.0, F32)

        linked = segcol == segrow
        bias_s[...] = jnp.where(linked & (row >= col), 0.0, -1e30)
        biast_s[...] = jnp.where(linked & (col >= row), 0.0, -1e30)
        leave = jnp.exp(last - cum) * jnp.where(segcol == seglast, 1.0, 0.0)
        lvs[...] = jnp.concatenate(split(leave, 2), axis=1)

        for g in range(GROUPS):
            part = slice(N * g, N * g + N)
            bt[g] = b_ref[:, part].astype(F32).T.astype(BF16)
            ct[g] = c_ref[:, part].astype(F32).T.astype(BF16)

        mine = c
        theirs = 1 - c

        def partner_copy(w, k):
            return remote(
                st.at[w, 2 * k + theirs], sp.at[w, k], dsend.at[w, k], drecv.at[w, k], (px, z, y, 1 - c)
            )

        def states(w, k, g):
            for s in range(4):
                q = 4 * g + s
                part = lanes_of(q, QL)
                both = indicator(q, 2)
                if w == 0:
                    factor = dot(lvs[...], both)
                    lexp[q] = factor
                    moved = (factor * x_ref[:, part].astype(F32)).astype(BF16)
                    xo[q] = moved
                    st[w, g, s] = dot(bt[g], moved).astype(BF16)
                else:
                    factor = dot(ens[...], both)
                    gr = grad[:, part].astype(F32)
                    moved = (factor * gr).astype(BF16)
                    gi[q] = moved
                    st[w, g, s] = dot(ct[g], moved).astype(BF16)
                    skp[q] = jnp.sum(gr * x_ref[:, part].astype(F32), axis=0, keepdims=True)

        def t_copy(w, k, off):
            other = lax.rem(y + off, NY)
            return remote(
                tt.at[w, k, other], tr.at[w, k, y], tsend.at[w, k, off - 1], trecv.at[w, k, off - 1], (px, z, other, c)
            )

        def chip_state(w, k):
            up, down = (0, 1) if w == 0 else (1, 0)
            partner_copy(w, k).wait_recv()
            g = 2 * k + mine
            for s in range(4):
                own = st[w, g, s].astype(F32)
                other = sp[w, k, s].astype(F32)
                first = jnp.where(c == up, own, other)
                second = jnp.where(c == up, other, own)
                decay = thx[g, s, pl.ds(2 * y + down, 1), :]
                tt[w, k, s] = (decay * first + second).astype(BF16)
            for off in range(1, NY):
                t_copy(w, k, off).start()
            tr[w, k, y] = tt[w, k, y]

        def chain_copy(w, k):
            step = 1 if w == 0 else nz - 1
            return remote(
                zs.at[w, k], zr.at[w, k], csend.at[w, k], crecv.at[w, k], (px, lax.rem(z + step, nz), y, c)
            )

        def e_copy(w, k, off):
            other = lax.rem(y + off, NY)
            return remote(
                es.at[w, k, other], er.at[w, k, y], esend.at[w, k, off - 1], erecv.at[w, k, off - 1], (px, z, other, c)
            )

        def chain(w, k):
            order = tuple(range(NY)) if w == 0 else tuple(reversed(range(NY)))
            first, final = (0, nz - 1) if w == 0 else (nz - 1, 0)
            g = 2 * k + mine
            for off in range(1, NY):
                t_copy(w, k, off).wait_recv()
            decay = [thx[g, y, 2 * i : 2 * i + 1, :] * thx[g, y, 2 * i + 1 : 2 * i + 2, :] for i in range(NY)]
            total = tr[w, k, order[0]].astype(F32)
            factor = decay[order[0]]
            for i in order[1:]:
                total = decay[i] * total + tr[w, k, i].astype(F32)
                factor = factor * decay[i]
            tz_s[...] = total

            @pl.when(z == first)
            def _():
                zr[w, k] = jnp.zeros((N, QL), BF16)

            @pl.when(z != first)
            def _():
                chain_copy(w, k).wait_recv()

            @pl.when(z != final)
            def _():
                zs[w, k] = (factor * zr[w, k].astype(F32) + tz_s[...]).astype(BF16)
                chain_copy(w, k).start()

            value = zr[w, k].astype(F32)
            for i in order:
                es[w, k, i] = value.astype(BF16)
                value = decay[i] * value + tr[w, k, i].astype(F32)
            for off in range(1, NY):
                e_copy(w, k, off).start()
            er[w, k, y] = es[w, k, y]

        def back_copy(w, k):
            return remote(epart.at[w, k], ex.at[w, k], psend.at[w, k], precv.at[w, k], (px, z, y, 1 - c))

        def hand_back(w, k):
            up = 0 if w == 0 else 1
            g = 2 * k + mine
            for off in range(1, NY):
                e_copy(w, k, off).wait_recv()
            for s in range(4):
                here = er[w, k, s]
                first = jnp.where(c == up, st[w, g, s].astype(F32), sp[w, k, s].astype(F32))
                decay = thx[g, s, pl.ds(2 * y + up, 1), :]
                after = decay * here.astype(F32) + first
                keep[w, k, s] = jnp.where(c == up, here.astype(F32), after).astype(BF16)
                epart[w, k, s] = jnp.where(c == up, after, here.astype(F32)).astype(BF16)
            back_copy(w, k).start()

        def fwd_states(k, carry):
            states(0, k, 2 * k + theirs)
            partner_copy(0, k).start()
            states(0, k, 2 * k + mine)
            return carry

        lax.fori_loop(0, PAIRS, fwd_states, 0)

        for off in range(1, 2 * NY):
            info_copy(off).wait_recv()

        @pl.when(z > 0)
        def _():
            remote(
                info_s, info_r.at[2 * NY], isend.at[7], irecv.at[7], (px, lax.rem(z + nz - 1, nz), y, c)
            ).wait_recv()

        th_s[...] = jnp.zeros((16, H), F32)
        for i in range(2 * NY):
            before = info_r[2 * NY if i == 0 else i - 1, 1:2, :]
            th_s[i : i + 1, :] = jnp.exp(info_r[i, 0:1, :]) * jnp.where(info_r[i, 1:2, :] == before, 1.0, 0.0)
        th_s[8:9, :] = skip_ref[...]
        enter_from = info_r[lax.rem(d + 2 * NY, 2 * NY + 1), 1:2, :]
        segc = jnp.broadcast_to(seg_ref[...].astype(F32), (T, T)).T
        enter = jnp.exp(cum_s[...]) * jnp.where(segc == enter_from, 1.0, 0.0)
        ens[...] = jnp.concatenate(split(enter, 2), axis=1)

        def table(g, carry):
            rows = jnp.concatenate(split(th_s[...], 3), axis=1)
            for s in range(4):
                thx[g, s] = dot(rows, indicator(4 * g + s, 3))
            return carry

        lax.fori_loop(0, GROUPS, table, 0)

        def fwd_chip(k, carry):
            chip_state(0, k)
            return carry

        lax.fori_loop(0, PAIRS, fwd_chip, 0)

        @pl.when(px == nx - 1)
        def _():
            keep_rows = jnp.broadcast_to(mask_ref[...].astype(F32), (T, T)).T
            wide = jnp.concatenate([keep_rows, keep_rows], axis=1)

            def body(q, carry):
                part = lanes_of(q, QL)
                grad[:, part] = (prev_ref[:, part].astype(F32) * wide).astype(BF16)
                return carry

            lax.fori_loop(0, QUARTERS, body, 0)

        def within(g):
            bg = b_ref[:, lanes_of(g, N)]
            cg = c_ref[:, lanes_of(g, N)]
            cross = dot_nt(bg, cg)
            cols = pltpu.roll(cum_s[...], lax.rem(H - 16 * g, H), 1)
            low = lax.broadcasted_iota(jnp.int32, (T, T), 1) < D
            total = jnp.zeros((T, T), F32)
            for j in range(8):
                part = pl.ds(pl.multiple_of(1024 * g + 128 * j, 128), 128)
                gp = grad[:, part]
                xp = x_ref[:, part]
                gf = gp.astype(F32)
                both = jnp.concatenate(
                    [jnp.where(low, gf, 0.0).astype(BF16), jnp.where(low, 0.0, gf).astype(BF16)], axis=0
                )
                prod = dot_nt(both, xp)
                pieces = []
                for i in range(2):
                    j2 = 2 * j + i
                    spread = cols[:, j2 : j2 + 1] - cumt_s[pl.ds(16 * g + j2, 1), :]
                    total = total + jnp.exp(spread + bias_s[...]) * prod[T * i : T * i + T, :]
                    pieces.append((jnp.exp(biast_s[...] - spread) * cross).astype(BF16))
                out = dot(jnp.concatenate(pieces, axis=1), both)
                half = slice(128 * (j % 2), 128 * (j % 2) + 128)
                gain = thx[g, j // 2, 8:9, half]
                gxa[4 * g + j // 2, :, half] = out + gain * gf
            gca[g] = dot(total.astype(BF16), bg)
            gba[g] = dot(total.T.astype(BF16), cg)

        def chains(w):
            def body(k, carry):
                chain(w, k)
                return carry

            lax.fori_loop(0, PAIRS, body, 0)

        def main(k, carry):
            @pl.when((k == 1) & (z < nz // 2))
            def _():
                chains(0)

            @pl.when((k == 2) & (z >= nz // 2))
            def _():
                chains(0)

            @pl.when(px < nx - 1)
            def _():
                grad_copy(k).wait_recv()

            states(1, k, 2 * k + theirs)
            partner_copy(1, k).start()
            states(1, k, 2 * k + mine)
            chip_state(1, k)
            within(2 * k)
            within(2 * k + 1)
            return carry

        lax.fori_loop(0, PAIRS, main, 0)

        row_q = lax.broadcasted_iota(jnp.int32, (QL, 128), 0)
        col_q = lax.broadcasted_iota(jnp.int32, (QL, 128), 1)
        pick = jnp.where(lax.shift_right_logical(row_q, 6) == col_q, 1.0, 0.0).astype(BF16)
        sums = jnp.reshape(skp[...], (QUARTERS, QL))
        sk_s[...] = sum(dot(piece, pick) for piece in split(sums, 3))
        sk_r[d] = sk_s[...]

        def sk_copy(off):
            return remote(sk_s, sk_r.at[d], ssend.at[off - 1], srecv.at[off - 1], plane_peer(off))

        def skz_copy(off):
            return remote(
                skz_s, skz_r.at[z], zsend.at[off - 1], zrecv.at[off - 1], (px, lax.rem(z + off, nz), y, c)
            )

        for off in range(1, 2 * NY):
            sk_copy(off).start()

        def fwd_back(k, carry):
            hand_back(0, k)
            return carry

        lax.fori_loop(0, PAIRS, fwd_back, 0)

        def finish_c(g, source, k):
            acc = gca[g]
            for s in range(4):
                acc = acc + dot_nt(gi[4 * g + s], source[0, k, s])
            gc_out[:, lanes_of(g, N)] = acc.astype(BF16)

        def finish_b(g, source, k):
            acc = gba[g]
            bg = b_ref[:, lanes_of(g, N)]
            for s in range(4):
                q = 4 * g + s
                later = source[1, k, s]
                acc = acc + dot_nt(xo[q], later)
                gx_out[:, lanes_of(q, QL)] = (gxa[q] + lexp[q] * dot(bg, later)).astype(BF16)
            gb_out[:, lanes_of(g, N)] = acc.astype(BF16)

        def end_c(k, carry):
            finish_c(2 * k + mine, keep, k)
            back_copy(0, k).wait_recv()
            finish_c(2 * k + theirs, ex, k)
            return carry

        chains(1)
        lax.fori_loop(0, PAIRS, end_c, 0)

        for off in range(1, 2 * NY):
            sk_copy(off).wait_recv()
        acc = sk_r[0]
        for i in range(1, 2 * NY):
            acc = acc + sk_r[i]
        skz_s[...] = acc
        skz_r[z] = acc
        for off in range(1, nz):
            skz_copy(off).start()

        def bwd_back(k, carry):
            hand_back(1, k)
            finish_b(2 * k + mine, keep, k)
            return carry

        lax.fori_loop(0, PAIRS, bwd_back, 0)

        def end_b(k, carry):
            back_copy(1, k).wait_recv()
            finish_b(2 * k + theirs, ex, k)
            return carry

        lax.fori_loop(0, PAIRS, end_b, 0)

        for off in range(1, nz):
            skz_copy(off).wait_recv()
        acc = skz_r[0]
        for i in range(1, nz):
            acc = acc + skz_r[i]
        sk_out[...] = acc

        @pl.when(px > 0)
        def _():
            for k in range(PAIRS):
                grad_copy(k).wait_send()

        for off in range(1, 2 * NY):
            info_copy(off).wait_send()
            sk_copy(off).wait_send()

        @pl.when((d == 2 * NY - 1) & (z < nz - 1))
        def _():
            for other in range(2 * NY):
                info_next(other).wait_send()

        for off in range(1, nz):
            skz_copy(off).wait_send()

        for w in range(2):
            final = nz - 1 if w == 0 else 0

            def drain(k, carry, w=w, final=final):
                partner_copy(w, k).wait_send()
                back_copy(w, k).wait_send()
                for off in range(1, NY):
                    t_copy(w, k, off).wait_send()
                    e_copy(w, k, off).wait_send()

                @pl.when(z != final)
                def _():
                    chain_copy(w, k).wait_send()

                return carry

            lax.fori_loop(0, PAIRS, drain, 0)

    return kernel


def call(nx, nz):
    vm = pltpu.VMEM
    dma = pltpu.SemaphoreType.DMA
    scratch = [
        vm((T, H * D), BF16),
        vm((QUARTERS, T, QL), BF16),
        vm((QUARTERS, T, QL), BF16),
        vm((QUARTERS, T, QL), F32),
        vm((QUARTERS, T, QL), F32),
        vm((GROUPS, T, N), F32),
        vm((GROUPS, T, N), F32),
        vm((T, H), F32),
        vm((H, T), F32),
        vm((T, T), F32),
        vm((T, T), F32),
        vm((T, 2 * H), BF16),
        vm((T, 2 * H), BF16),
        vm((GROUPS, N, T), BF16),
        vm((GROUPS, N, T), BF16),
        vm((8, H), F32),
        vm((2 * NY + 1, 8, H), F32),
        vm((16, H), F32),
        vm((GROUPS, 4, 16, QL), F32),
        vm((2, GROUPS, 4, N, QL), BF16),
        vm((2, PAIRS, 4, N, QL), BF16),
        vm((2, PAIRS, NY, N, QL), BF16),
        vm((2, PAIRS, NY, N, QL), BF16),
        vm((2, PAIRS, N, QL), BF16),
        vm((2, PAIRS, N, QL), BF16),
        vm((2, PAIRS, NY, N, QL), BF16),
        vm((2, PAIRS, NY, N, QL), BF16),
        vm((2, PAIRS, 4, N, QL), BF16),
        vm((2, PAIRS, 4, N, QL), BF16),
        vm((2, PAIRS, 4, N, QL), BF16),
        vm((N, QL), F32),
        vm((QUARTERS, 1, QL), F32),
        vm((QUARTERS, 128), F32),
        vm((2 * NY, QUARTERS, 128), F32),
        vm((QUARTERS, 128), F32),
        vm((nz, QUARTERS, 128), F32),
        dma((PAIRS,)), dma((PAIRS,)),
        dma((7 + 2 * NY,)), dma((8,)),
        dma((7,)), dma((7,)),
        dma((nz - 1,)), dma((nz - 1,)),
        dma((2, PAIRS)), dma((2, PAIRS)),
        dma((2, PAIRS, NY - 1)), dma((2, PAIRS, NY - 1)),
        dma((2, PAIRS)), dma((2, PAIRS)),
        dma((2, PAIRS, NY - 1)), dma((2, PAIRS, NY - 1)),
        dma((2, PAIRS)), dma((2, PAIRS)),
    ]
    return pl.pallas_call(
        make_kernel(nx, nz),
        out_shape=(
            jax.ShapeDtypeStruct((T, H * D), BF16),
            jax.ShapeDtypeStruct((T, GROUPS * N), BF16),
            jax.ShapeDtypeStruct((T, GROUPS * N), BF16),
            jax.ShapeDtypeStruct((QUARTERS, 128), F32),
        ),
        in_specs=[pl.BlockSpec(memory_space=pltpu.VMEM)] * 9,
        out_specs=[pl.BlockSpec(memory_space=pltpu.VMEM)] * 4,
        scratch_shapes=scratch,
        compiler_params=pltpu.CompilerParams(vmem_limit_bytes=62 * 2**20),
        name="mixer_backward",
    )


def on_device(previous, saved_head_inputs, input_b, input_c, steps, decay_rate, skip_gain, segment_ids, advantage_mask):
    kernel = call(lax.axis_size("pipe"), lax.axis_size("seq_0"))
    gx, gb, gc, sk = kernel(
        previous[0],
        saved_head_inputs[0],
        input_b[0],
        input_c[0],
        steps[0],
        decay_rate,
        skip_gain,
        segment_ids,
        advantage_mask[None],
    )
    return gx[None], gb[None], gc[None], sk[:, :4].reshape(1, H)


def solution(mesh):
    finer = Mesh(
        mesh.devices.reshape(mesh.shape["pipe"], mesh.shape["seq"] // (2 * NY), NY, 2),
        ("pipe", "seq_0", "seq_1", "seq_2"),
    )
    return jax.shard_map(
        on_device,
        mesh=finer,
        in_specs=(
            P("pipe", SEQ, None),
            P("pipe", SEQ, None),
            P("pipe", SEQ, None),
            P("pipe", SEQ, None),
            P("pipe", SEQ, None),
            P("pipe", None),
            P("pipe", None),
            P("pipe", SEQ),
            P(SEQ),
        ),
        out_specs=(
            P("pipe", SEQ, None),
            P("pipe", SEQ, None),
            P("pipe", SEQ, None),
            P("pipe", None),
        ),
        check_vma=False,
    )
```

time: 635 us -> 123 us (0.19); the launches traced: 628 us -> 122 us
  waiting for transfers between devices: 195 us -> 0 us
  local copies, waits for them, and re-layouts: 190 us -> 5.9 us
  Pallas kernels: 0 us -> 116 us
  other arithmetic: 73 us -> 0 us
  starting transfers between devices: 65.8 us -> 0 us
  matrix products: 61 us -> 0 us
  blocking collectives: 35.7 us -> 0 us
    ppermute x18 -> x0, waiting for transfers between devices: 185 us -> none  [the longest x9 124 us: swapped(): return lax.ppermute(block, axis, route)]
    pallas_call x0 -> x1, Pallas kernels: none -> 116 us  [on_device(): kernel(previous[0], saved_head_inputs[0], input_b[0], input_c[0], steps[0...]
    dynamic_update_slice x22 -> x0, local copies, waits for them, and re-layouts: 76.1 us -> none  [the longest x6 75.3 us: butterfly(): lax.dynamic_update_index_in_dim(view, jnp.expand_dims(received, 1), 1 - m...]
    dot_general x40 -> x0, matrix products: 61 us -> none  [mix(): return jnp.einsum(form, left, right, preferred_element_type=jnp.float32)]
    ppermute x18 -> x0, starting transfers between devices: 40.9 us -> none  [the longest x9 26.8 us: from_behind(): lax.ppermute(value, axis, [(source, source + steps) for source in range(i...]
    psum x3 -> x0, blocking collectives: 35.7 us -> none  [one_axis_at_a_time(): shard = lax.psum(shard, axis)]
    all_to_all x2 -> x0, starting transfers between devices: 24.9 us -> none  [copy_for_each(): return lax.all_to_all(copies, axis, split_axis=0, concat_axis=0, tiled=True)]
    dynamic_slice x16 -> x0, local copies, waits for them, and re-layouts: 19.2 us -> none  [the longest x4 16.2 us: butterfly(): half = lax.dynamic_index_in_dim(view, 1 - mine, 1, keepdims=False)]
  transfers between devices with their start and end apart: 20 -> 0, of which waited for: 12 -> 0; matrix products, arithmetic and copies ran while one was open for 5% -> 0% of each run, Pallas kernels for 0% -> 0%
where the time goes in v1:
time: 123 us; the launch traced here: 122 us
  Pallas kernels  116 us (94%)
  local copies, waits for them, and re-layouts  5.9 us (5%)
    pallas_call x1, Pallas kernels, on_device(): kernel(previous[0], saved_head_inputs[0], input_b[0], input_c[0], steps[0...  116 us
    unnamed x7, local copies, waits for them, and re-layouts  4.56 us

profile of v1, /device:TPU:1, one launch (start us, length us, event | category | flops | bytes accessed | tf_op | source)
XLA Modules:
  0.0 122.1 jit_solution(15740985864458295961)
XLA Ops:
  0.6 115.5 %mixer_backward.1 = (bf16[128,8192]{1,0:T(8,128)(2,1)}, bf16[128,1024]{1,0:T(8,128)(2,1)}, bf16[128,1024]{1,0:T(8,128)(2,1)}, f32[32,128]{1,0:T(8,128)}) custom-call(bf16[128,8192]{1,0:T(8,128)(2,1)} %bitcast.10, bf16[128,8192]{1,0:T(8,128)(2,1)} %bitcast.11, bf16[128,1024]{1,0:T(8,128)(2,1)} %bitcast.13, bf16[128,1024]{1,0:T(8,128)(2,1)} %bitcast.14, ...), custom_call_target="tpu_custom_call" | custom-call | tf_op jit(solution)/shard_map/mixer_backward/pallas_call | solution.py:546
  116.2 1.3 %reshape.11 = f32[1,128]{1,0:T(1,128)} reshape(f32[32,4]{1,0:T(8,128)} %bitcast.18) | data formatting | bytes 1024 | tf_op jit(solution)/shard_map/reshape | solution.py:557
  117.5 0.0 copy-start.1
  117.5 0.0 copy-start
  117.5 3.2 %copy.16 = bf16[1,128,8192]{2,1,0:T(8,128)(2,1)} copy(bf16[1,128,8192]{2,1,0:T(8,128)(2,1)} %bitcast.12) | data formatting | bytes 4194304
  120.7 0.0 copy-done.1
  120.7 0.7 copy.17
  121.4 0.0 copy-done
  121.4 0.7 copy.18
Async XLA Ops:
  117.5 3.2 %copy-start.1 = (bf16[128,1024]{1,0:T(8,128)(2,1)S(1)}, bf16[128,1024]{1,0:T(8,128)(2,1)}, u32[]{:S(2)}) copy-start(bf16[128,1024]{1,0:T(8,128)(2,1)} %get-tuple-element.9) | copy-start | bytes 786436
  117.5 3.9 %copy-start = (bf16[128,1024]{1,0:T(8,128)(2,1)S(1)}, bf16[128,1024]{1,0:T(8,128)(2,1)}, u32[]{:S(2)}) copy-start(bf16[128,1024]{1,0:T(8,128)(2,1)} %get-tuple-element.10) | copy-start | bytes 786436

commit v2 on v1

v2 whole, which is shorter than its diff:
```python
import jax
import jax.numpy as jnp
from jax import lax
from jax.experimental import pallas as pl
from jax.experimental.pallas import tpu as pltpu
from jax.sharding import Mesh
from jax.sharding import PartitionSpec as P

SEQ = ("seq_0", "seq_1", "seq_2")
MESH = pl.DeviceIdType.MESH
F32 = jnp.float32
BF16 = jnp.bfloat16
NY = 4
T = 128
N = 128
H = 128
D = 64
GROUPS = 8
CHUNKS = 8
MINE = 2 * CHUNKS
ROWS = N // NY
QL = 256
QUARTERS = 32


def split(v, parts):
    out = []
    for _ in range(parts):
        piece = v.astype(BF16)
        out.append(piece)
        v = v - piece.astype(F32)
    return out


def dot(a, b):
    return lax.dot_general(a, b, (((1,), (0,)), ((), ())), preferred_element_type=F32)


def dot_nt(a, b):
    return lax.dot_general(a, b, (((1,), (1,)), ((), ())), preferred_element_type=F32)


def lanes_of(index, width):
    return pl.ds(pl.multiple_of(index * width, width), width)


def indicator(q, copies):
    row = lax.broadcasted_iota(jnp.int32, (H, QL), 0)
    col = lax.broadcasted_iota(jnp.int32, (H, QL), 1)
    one = jnp.where(row == 4 * q + lax.shift_right_logical(col, 6), 1.0, 0.0).astype(BF16)
    return jnp.concatenate([one] * copies, axis=0)


def make_kernel(nx, nz):
    width = (4, 2)
    count = (MINE // 4, CHUNKS)

    def kernel(
        prev_ref, x_ref, b_ref, c_ref, steps_ref, rate_ref, skip_ref, seg_ref, mask_ref,
        gx_out, gb_out, gc_out, sk_out,
        grad, xo, gi, gxa, lexp, gca, gba, cum_s, cumt_s, bias_s, biast_s, eexp, lvs, bt, ct, wide_s, fz_s, fz_r, fzx,
        info_s, info_r, th_s, thx,
        st, sp, tt, t1, us, u2, zs, zr, az, ho, hi, vo, vi, eo, er, keep, epart, ex, tz_s,
        skp, sk_s, sk_r, skz_s, skz_r,
        gsend, grecv, isend, irecv, ssend, srecv, zsend, zrecv,
        fsend, frecv, asend, arecv, hsend, hrecv, dsend, drecv, t1send, t1recv, u2send, u2recv, csend, crecv, v2send, v2recv, e1send, e1recv, psend, precv,
    ):
        px = lax.axis_index("pipe")
        z = lax.axis_index("seq_0")
        y = lax.axis_index("seq_1")
        c = lax.axis_index("seq_2")
        d = 2 * y + c
        last_d = 2 * NY - 1

        def remote(src, dst, ssem, rsem, where):
            return pltpu.make_async_remote_copy(
                src_ref=src, dst_ref=dst, send_sem=ssem, recv_sem=rsem, device_id=where, device_id_type=MESH
            )

        def plane_peer(off):
            other = lax.rem(d + off, 2 * NY)
            return (px, z, lax.div(other, 2), lax.rem(other, 2))

        def z_peer(off):
            return (px, lax.rem(z + off, nz), y, c)

        barrier = pltpu.get_barrier_semaphore()

        def greet(where):
            pl.semaphore_signal(barrier, inc=1, device_id=where, device_id_type=MESH)

        for off in range(1, 2 * NY):
            greet(plane_peer(off))
        for off in range(1, nz):
            greet(z_peer(off))

        @pl.when(px < nx - 1)
        def _():
            greet((lax.rem(px + 1, nx), z, y, c))

        @pl.when(z > 0)
        def _():
            greet((px, lax.rem(z + nz - 1, nz), NY - 1, 1))

        from_next = (d == last_d) & (z < nz - 1)
        callers = 2 * NY - 1 + nz - 1 + jnp.where(px > 0, 1, 0) + jnp.where(from_next, 2 * NY, 0)
        pl.semaphore_wait(barrier, callers)

        def grad_copy(k):
            part = lanes_of(k, 4 * QL)
            return remote(
                prev_ref.at[:, part], grad.at[:, part], gsend.at[k], grecv.at[k], (lax.rem(px + nx - 1, nx), z, y, c)
            )

        @pl.when(px > 0)
        def _():
            def body(k, carry):
                grad_copy(k).start()
                return carry

            lax.fori_loop(0, CHUNKS, body, 0)

        row = lax.broadcasted_iota(jnp.int32, (T, T), 0)
        col = lax.broadcasted_iota(jnp.int32, (T, T), 1)
        cum = -(steps_ref[...] * rate_ref[...])
        for shift in (1, 2, 4, 8, 16, 32, 64):
            cum = cum + jnp.where(row >= shift, pltpu.roll(cum, shift, 0), 0.0)
        cum_s[...] = cum
        cumt_s[...] = cum.T
        last = cum[T - 1 : T, :]
        segrow = jnp.broadcast_to(seg_ref[...].astype(F32), (T, T))
        segcol = segrow.T
        seglast = segcol[T - 1 : T, :]
        info_s[0:1, :] = last
        info_s[1:2, :] = seglast
        info_s[2:8, :] = jnp.zeros((6, H), F32)
        info_r[d] = info_s[...]

        def info_copy(off):
            return remote(info_s, info_r.at[d], isend.at[off - 1], irecv.at[off - 1], plane_peer(off))

        def info_next(other):
            return remote(
                info_s, info_r.at[2 * NY], isend.at[7 + other], irecv.at[7], (px, lax.rem(z + 1, nz), other // 2, other % 2)
            )

        for off in range(1, 2 * NY):
            info_copy(off).start()

        @pl.when((d == last_d) & (z < nz - 1))
        def _():
            for other in range(2 * NY):
                info_next(other).start()

        @pl.when(z == 0)
        def _():
            info_r[2 * NY] = jnp.full((8, H), -1.0, F32)

        linked = segcol == segrow
        bias_s[...] = jnp.where(linked & (row >= col), 0.0, -1e30)
        biast_s[...] = jnp.where(linked & (col >= row), 0.0, -1e30)
        leave = jnp.exp(last - cum) * jnp.where(segcol == seglast, 1.0, 0.0)
        lvs[...] = jnp.concatenate(split(leave, 2), axis=1)
        kept = jnp.broadcast_to(mask_ref[...].astype(F32), (T, T)).T
        wide_s[...] = jnp.concatenate([kept, kept], axis=1)

        for g in range(GROUPS):
            part = slice(N * g, N * g + N)
            bt[g] = b_ref[:, part].astype(F32).T.astype(BF16)
            ct[g] = c_ref[:, part].astype(F32).T.astype(BF16)

        pair = lax.div(y, 2)
        low_y = lax.rem(y, 2)
        half_of = jnp.where(low_y == pair, 0, 1)
        in_pair = (px, z, 2 * pair + 1 - low_y, c)
        over_pairs = (px, z, NY - 1 - y, c)

        mine = c
        theirs = 1 - c

        def some(ref, w, k):
            return ref.at[w, pl.ds(width[w] * k, width[w])]

        def partner_copy(w, k):
            n = width[w]
            return remote(
                st.at[w, theirs, pl.ds(n * k, n)], some(sp, w, k), dsend.at[w, k], drecv.at[w, k], (px, z, y, 1 - c)
            )

        def quarter(m, side):
            return 4 * lax.div(m, 2) + 2 * side + lax.rem(m, 2)

        def states(w, k, side):
            for i in range(width[w]):
                m = width[w] * k + i
                q = quarter(m, side)
                g = lax.div(m, 2)
                part = lanes_of(q, QL)
                if w == 0:
                    factor = dot(lvs[...], indicator(q, 2))
                    lexp[q] = factor
                    moved = (factor * x_ref[:, part].astype(F32)).astype(BF16)
                    xo[q] = moved
                    st[w, side, m] = dot(bt[g], moved).astype(BF16)
                else:
                    gr = grad[:, part].astype(F32)
                    moved = (eexp[q] * gr).astype(BF16)
                    gi[q] = moved
                    st[w, side, m] = dot(ct[g], moved).astype(BF16)
                    skp[q] = jnp.sum(gr * x_ref[:, part].astype(F32), axis=0, keepdims=True)

        def t_copy(w, k):
            m = pl.ds(width[w] * k, width[w])
            return remote(tt.at[w, m, 1 - half_of], t1.at[w, m], t1send.at[w, k], t1recv.at[w, k], in_pair)

        def u_copy(w, k):
            m = pl.ds(width[w] * k, width[w])
            return remote(us.at[w, m, 1 - pair], u2.at[w, m], u2send.at[w, k], u2recv.at[w, k], over_pairs)

        def v_copy(w, k):
            m = pl.ds(width[w] * k, width[w])
            return remote(vo.at[w, m], vi.at[w, m, pair], v2send.at[w, k], v2recv.at[w, k], over_pairs)

        def e_copy(w, k):
            m = pl.ds(width[w] * k, width[w])
            return remote(eo.at[w, m], er.at[w, m, half_of], e1send.at[w, k], e1recv.at[w, k], in_pair)

        def chip_decay(q, chip):
            return thx[q, pl.ds(2 * chip, 1), :] * thx[q, pl.ds(2 * chip + 1, 1), :]

        def pair_decay(q, which):
            return chip_decay(q, 2 * which) * chip_decay(q, 2 * which + 1)

        def chip_state(w, k):
            up, down = (0, 1) if w == 0 else (1, 0)
            partner_copy(w, k).wait_recv()
            for i in range(width[w]):
                m = width[w] * k + i
                own = st[w, mine, m].astype(F32)
                other = sp[w, m].astype(F32)
                first = jnp.where(c == up, own, other)
                second = jnp.where(c == up, other, own)
                decay = thx[quarter(m, mine), pl.ds(2 * y + down, 1), :]
                tt[w, m] = (decay * first + second).astype(BF16).reshape(2, 2 * ROWS, QL)
            t_copy(w, k).start()

        def pair_first(w, m):
            own = tt[w, m, half_of].astype(F32)
            other = t1[w, m].astype(F32)
            return jnp.where(low_y == w, own, other), jnp.where(low_y == w, other, own)

        def pair_step(w, k):
            t_copy(w, k).wait_recv()
            for i in range(width[w]):
                m = width[w] * k + i
                first, second = pair_first(w, m)
                decay = chip_decay(quarter(m, mine), 2 * pair + 1 - w)
                us[w, m] = (decay * first + second).astype(BF16).reshape(2, ROWS, QL)
            u_copy(w, k).start()

        def plane_first(w, m):
            own = us[w, m, pair].astype(F32)
            other = u2[w, m].astype(F32)
            return jnp.where(pair == w, own, other), jnp.where(pair == w, other, own)

        def chain_copy(k):
            m = pl.ds(width[0] * k, width[0])
            return remote(zs.at[m], zr.at[m], csend.at[k], crecv.at[k], z_peer(1))

        def across(k, other):
            m = pl.ds(width[1] * k, width[1])
            return remote(az.at[z, m], az.at[z, m], asend.at[k, other], arecv.at[k, z], (px, other, y, c))

        half = nz // 2
        start = half * lax.div(z, half)

        def down(k, other):
            m = pl.ds(width[1] * k, width[1])
            return remote(ho.at[m], hi.at[m], hsend.at[k, other], hrecv.at[k], (px, other, y, c))

        def arrived(k, source):
            m = pl.ds(width[1] * k, width[1])
            return remote(az.at[source, m], az.at[source, m], asend.at[k, source], arecv.at[k, source], (px, source, y, c))

        def plane_total(w, m):
            q = quarter(m, mine)
            first, second = plane_first(w, m)
            decay = pair_decay(q, 1 - w)
            return decay * first + second, decay * pair_decay(q, w)

        def spread_out(w, k, values):
            for i, value in enumerate(values):
                m = width[w] * k + i
                after = pair_decay(quarter(m, mine), w) * value + plane_first(w, m)[0]
                vi[w, m, pair] = jnp.where(pair == w, value, after).astype(BF16)
                vo[w, m] = jnp.where(pair == w, after, value).astype(BF16)
            v_copy(w, k).start()

        def pair_out(w, k):
            v_copy(w, k).wait_recv()
            for i in range(width[w]):
                m = width[w] * k + i
                value = vi[w, m].reshape(2 * ROWS, QL).astype(F32)
                after = chip_decay(quarter(m, mine), 2 * pair + w) * value + pair_first(w, m)[0]
                er[w, m, half_of] = jnp.where(low_y == w, value, after).astype(BF16)
                eo[w, m] = jnp.where(low_y == w, after, value).astype(BF16)
            e_copy(w, k).start()

        def chain(k):
            u_copy(0, k).wait_recv()
            held = []
            for i in range(width[0]):
                m = width[0] * k + i
                total, factor = plane_total(0, m)
                tz_s[i] = total
                held.append((m, factor))

            @pl.when(z == 0)
            def _():
                for m, _factor in held:
                    zr[m] = jnp.zeros((ROWS, QL), BF16)

            @pl.when(z > 0)
            def _():
                chain_copy(k).wait_recv()

            @pl.when(z < nz - 1)
            def _():
                for i, (m, factor) in enumerate(held):
                    zs[m] = (factor * zr[m].astype(F32) + tz_s[i]).astype(BF16)
                chain_copy(k).start()

            spread_out(0, k, [zr[m].astype(F32) for m, _factor in held])

        def plane_send(k):
            u_copy(1, k).wait_recv()
            for i in range(width[1]):
                m = width[1] * k + i
                az[z, m] = plane_total(1, m)[0].astype(BF16)

            def body(other, carry):
                across(k, other).start()
                return carry

            lax.fori_loop(start, z, body, 0)

        def plane_back(k):
            @pl.when(z >= half)
            def _():
                for i in range(width[1]):
                    tz_s[i] = jnp.zeros((ROWS, QL), F32)

            @pl.when(z < half)
            def _():
                down(k, half).wait_recv()
                for i in range(width[1]):
                    tz_s[i] = hi[width[1] * k + i].astype(F32)

            def body(t, carry):
                source = start + half - 1 - t
                arrived(k, source).wait_recv()
                for i in range(width[1]):
                    m = width[1] * k + i
                    factor = fzx[quarter(m, mine), pl.ds(source, 1), :]
                    tz_s[i] = factor * tz_s[i] + az[source, m].astype(F32)
                return carry

            lax.fori_loop(0, start + half - 1 - z, body, 0)

            @pl.when(z == half)
            def _():
                for i in range(width[1]):
                    m = width[1] * k + i
                    total, factor = plane_total(1, m)
                    ho[m] = (factor * tz_s[i] + total).astype(BF16)
                for other in range(half):
                    down(k, other).start()

            spread_out(1, k, [tz_s[i] for i in range(width[1])])

        def back_copy(w, k):
            return remote(some(epart, w, k), some(ex, w, k), psend.at[w, k], precv.at[w, k], (px, z, y, 1 - c))

        def hand_back(w, k):
            up = 0 if w == 0 else 1
            e_copy(w, k).wait_recv()
            for i in range(width[w]):
                m = width[w] * k + i
                here = er[w, m].reshape(N, QL).astype(F32)
                first = jnp.where(c == up, st[w, mine, m].astype(F32), sp[w, m].astype(F32))
                decay = thx[quarter(m, mine), pl.ds(2 * y + up, 1), :]
                after = decay * here + first
                keep[w, m] = jnp.where(c == up, here, after).astype(BF16)
                epart[w, m] = jnp.where(c == up, after, here).astype(BF16)
            back_copy(w, k).start()

        def finish_c(k):
            back_copy(0, k).wait_recv()
            for j in range(2):
                g = 2 * k + j
                acc = gca[g]
                for i in range(2):
                    m = 2 * g + i
                    acc = acc + dot_nt(gi[quarter(m, mine)], keep[0, m]) + dot_nt(gi[quarter(m, theirs)], ex[0, m])
                gc_out[:, lanes_of(g, N)] = acc.astype(BF16)

        def finish_b(g):
            back_copy(1, g).wait_recv()
            bg = b_ref[:, lanes_of(g, N)]
            acc = gba[g]
            for side, source in ((mine, keep), (theirs, ex)):
                for i in range(2):
                    m = 2 * g + i
                    q = quarter(m, side)
                    later = source[1, m]
                    acc = acc + dot_nt(xo[q], later)
                    gx_out[:, lanes_of(q, QL)] = (gxa[q] + lexp[q] * dot(bg, later)).astype(BF16)
            gb_out[:, lanes_of(g, N)] = acc.astype(BF16)

        def fwd_states(k, carry):
            states(0, k, theirs)
            partner_copy(0, k).start()
            states(0, k, mine)
            return carry

        lax.fori_loop(0, count[0], fwd_states, 0)

        for off in range(1, 2 * NY):
            info_copy(off).wait_recv()

        @pl.when(z > 0)
        def _():
            remote(info_s, info_r.at[2 * NY], isend.at[7], irecv.at[7], z_peer(nz - 1)).wait_recv()

        th_s[...] = jnp.zeros((16, H), F32)
        for i in range(2 * NY):
            before = info_r[2 * NY if i == 0 else i - 1, 1:2, :]
            th_s[i : i + 1, :] = jnp.exp(info_r[i, 0:1, :]) * jnp.where(info_r[i, 1:2, :] == before, 1.0, 0.0)
        th_s[8:9, :] = skip_ref[...]
        enter_from = info_r[lax.rem(d + 2 * NY, 2 * NY + 1), 1:2, :]
        segc = jnp.broadcast_to(seg_ref[...].astype(F32), (T, T)).T
        enter = jnp.exp(cum_s[...]) * jnp.where(segc == enter_from, 1.0, 0.0)
        lvs[...] = jnp.concatenate(split(enter, 2), axis=1)
        whole = th_s[0:1, :]
        for i in range(1, 2 * NY):
            whole = whole * th_s[i : i + 1, :]
        fz_s[...] = jnp.broadcast_to(whole, (8, H))
        fz_r[z] = fz_s[...]

        def f_copy(other):
            return remote(fz_s, fz_r.at[z], fsend.at[other], frecv.at[z], (px, other, y, c))

        def f_arrived(source):
            return remote(fz_s, fz_r.at[source], fsend.at[source], frecv.at[source], (px, source, y, c))

        def f_start(other, carry):
            f_copy(other).start()
            return carry

        lax.fori_loop(0, z, f_start, 0)

        def table(k, carry):
            rows = jnp.concatenate(split(th_s[...], 3), axis=1)
            for i in range(4):
                thx[4 * k + i] = dot(rows, indicator(4 * k + i, 3))
            return carry

        lax.fori_loop(0, QUARTERS // 4, table, 0)

        def fwd_chip(k, carry):
            chip_state(0, k)
            return carry

        lax.fori_loop(0, count[0], fwd_chip, 0)

        def enter_wide(k, carry):
            for i in range(4):
                eexp[4 * k + i] = dot(lvs[...], indicator(4 * k + i, 2))
            return carry

        enter_wide(0, 0)

        def f_wait(t, carry):
            f_arrived(nz - 1 - t).wait_recv()
            return carry

        def plane_table():
            lax.fori_loop(0, nz - 1 - z, f_wait, 0)
            everything = jnp.concatenate(
                [jnp.where(i > z, fz_r[i, 0:1, :], 0.0) for i in range(nz)], axis=0
            )
            th_s[0:nz, :] = everything

            def body(k, carry):
                rows = jnp.concatenate(split(th_s[...], 3), axis=1)
                for i in range(4):
                    fzx[4 * k + i] = dot(rows, indicator(4 * k + i, 3))
                return carry

            lax.fori_loop(0, QUARTERS // 4, body, 0)

        def within(g):
            bg = b_ref[:, lanes_of(g, N)]
            cg = c_ref[:, lanes_of(g, N)]
            cross = dot_nt(bg, cg)
            cols = pltpu.roll(cum_s[...], lax.rem(H - 16 * g, H), 1)
            low = lax.broadcasted_iota(jnp.int32, (T, T), 1) < D
            total = jnp.zeros((T, T), F32)
            for j in range(8):
                part = pl.ds(pl.multiple_of(1024 * g + 128 * j, 128), 128)
                gf = grad[:, part].astype(F32)
                xp = x_ref[:, part]
                both = jnp.concatenate(
                    [jnp.where(low, gf, 0.0).astype(BF16), jnp.where(low, 0.0, gf).astype(BF16)], axis=0
                )
                prod = dot_nt(both, xp)
                pieces = []
                for i in range(2):
                    j2 = 2 * j + i
                    spread = cols[:, j2 : j2 + 1] - cumt_s[pl.ds(16 * g + j2, 1), :]
                    total = total + jnp.exp(spread + bias_s[...]) * prod[T * i : T * i + T, :]
                    pieces.append((jnp.exp(biast_s[...] - spread) * cross).astype(BF16))
                out = dot(jnp.concatenate(pieces, axis=1), both)
                half = slice(128 * (j % 2), 128 * (j % 2) + 128)
                q = 4 * g + j // 2
                gxa[q, :, half] = out + thx[q, 8:9, half] * gf
            gca[g] = dot(total.astype(BF16), bg)
            gba[g] = dot(total.T.astype(BF16), cg)

        def sk_copy(off):
            return remote(sk_s, sk_r.at[d], ssend.at[off - 1], srecv.at[off - 1], plane_peer(off))

        def skz_copy(off):
            return remote(skz_s, skz_r.at[z], zsend.at[off - 1], zrecv.at[off - 1], z_peer(off))

        def sk_plane():
            row_q = lax.broadcasted_iota(jnp.int32, (QL, 128), 0)
            col_q = lax.broadcasted_iota(jnp.int32, (QL, 128), 1)
            pick = jnp.where(lax.shift_right_logical(row_q, 6) == (col_q & 3), 1.0, 0.0).astype(BF16)
            sums = jnp.reshape(skp[...], (QUARTERS, QL))
            heads = sum(dot(piece, pick) for piece in split(sums, 3))
            own_row = lax.broadcasted_iota(jnp.int32, (QUARTERS, 128), 0)
            own_col = lax.broadcasted_iota(jnp.int32, (QUARTERS, 128), 1)
            heads = jnp.where(lax.shift_right_logical(own_col, 2) == own_row, heads, 0.0)
            sk_s[...] = jnp.broadcast_to(jnp.sum(heads, axis=0, keepdims=True), (8, 128))
            sk_r[d] = sk_s[...]
            for off in range(1, 2 * NY):
                sk_copy(off).start()

        def sk_along():
            for off in range(1, 2 * NY):
                sk_copy(off).wait_recv()
            acc = sk_r[0]
            for i in range(1, 2 * NY):
                acc = acc + sk_r[i]
            skz_s[...] = acc
            skz_r[z] = acc
            for off in range(1, nz):
                skz_copy(off).start()

        def each(n, step):
            def body(k, carry):
                step(k)
                return carry

            lax.fori_loop(0, n, body, 0)

        chain_at = 2 + lax.div(z * 5 + 3, nz - 1)
        back_at = jnp.where(z < half, 4, 3)

        def main(k, carry):
            def at(lag, n, step):
                @pl.when((k >= lag) & (k < lag + n))
                def _():
                    step(k - lag)

            def begin(k):
                @pl.when(px == nx - 1)
                def _():
                    for i in range(4):
                        part = lanes_of(4 * k + i, QL)
                        grad[:, part] = (prev_ref[:, part].astype(F32) * wide_s[...]).astype(BF16)

                @pl.when(px < nx - 1)
                def _():
                    grad_copy(k).wait_recv()

                states(1, k, theirs)
                partner_copy(1, k).start()
                states(1, k, mine)

                @pl.when(k < CHUNKS - 1)
                def _():
                    enter_wide(k + 1, 0)

                chip_state(1, k)
                within(k)

            at(0, CHUNKS, begin)

            @pl.when(k == 1)
            def _():
                plane_table()

            @pl.when(k == CHUNKS)
            def _():
                sk_plane()

            at(1, count[1], lambda i: pair_step(1, i))
            at(2, count[1], plane_send)
            at(back_at, count[1], plane_back)
            at(back_at + 1, count[1], lambda i: pair_out(1, i))
            at(back_at + 2, count[1], lambda i: hand_back(1, i))

            @pl.when(k == CHUNKS + 2)
            def _():
                sk_along()

            at(back_at + 3, count[1], finish_b)
            at(1, count[0], lambda i: pair_step(0, i))
            at(chain_at, count[0], chain)
            at(chain_at + 1, count[0], lambda i: pair_out(0, i))
            at(chain_at + 2, count[0], lambda i: hand_back(0, i))
            at(chain_at + 3, count[0], finish_c)
            return carry

        lax.fori_loop(0, CHUNKS + 7, main, 0)

        for off in range(1, nz):
            skz_copy(off).wait_recv()
        acc = skz_r[0]
        for i in range(1, nz):
            acc = acc + skz_r[i]
        sk_out[...] = acc[0:1, :]

        @pl.when(px > 0)
        def _():
            def body(k, carry):
                grad_copy(k).wait_send()
                return carry

            lax.fori_loop(0, CHUNKS, body, 0)

        for off in range(1, 2 * NY):
            info_copy(off).wait_send()
            sk_copy(off).wait_send()

        @pl.when((d == last_d) & (z < nz - 1))
        def _():
            for other in range(2 * NY):
                info_next(other).wait_send()

        for off in range(1, nz):
            skz_copy(off).wait_send()

        for w in range(2):

            def drain(k, w=w):
                partner_copy(w, k).wait_send()
                back_copy(w, k).wait_send()
                t_copy(w, k).wait_send()
                u_copy(w, k).wait_send()
                v_copy(w, k).wait_send()
                e_copy(w, k).wait_send()
                if w == 0:

                    @pl.when(z < nz - 1)
                    def _():
                        chain_copy(k).wait_send()
                else:

                    def let_go(other, carry, k=k):
                        across(k, other).wait_send()
                        return carry

                    lax.fori_loop(start, z, let_go, 0)

                    @pl.when(z == half)
                    def _():
                        for other in range(half):
                            down(k, other).wait_send()


            each(count[w], drain)
        each(z, lambda other: f_copy(other).wait_send())

    return kernel


def call(nx, nz):
    vm = pltpu.VMEM
    dma = pltpu.SemaphoreType.DMA
    scratch = [
        vm((T, H * D), BF16),
        vm((QUARTERS, T, QL), BF16),
        vm((QUARTERS, T, QL), BF16),
        vm((QUARTERS, T, QL), F32),
        vm((QUARTERS, T, QL), F32),
        vm((GROUPS, T, N), F32),
        vm((GROUPS, T, N), F32),
        vm((T, H), F32),
        vm((H, T), F32),
        vm((T, T), F32),
        vm((T, T), F32),
        vm((QUARTERS, T, QL), F32),
        vm((T, 2 * H), BF16),
        vm((GROUPS, N, T), BF16),
        vm((GROUPS, N, T), BF16),
        vm((T, QL), F32),
        vm((8, H), F32),
        vm((nz, 8, H), F32),
        vm((QUARTERS, 16, QL), F32),
        vm((8, H), F32),
        vm((2 * NY + 1, 8, H), F32),
        vm((16, H), F32),
        vm((QUARTERS, 16, QL), F32),
        vm((2, 2, MINE, N, QL), BF16),
        vm((2, MINE, N, QL), BF16),
        vm((2, MINE, 2, 2 * ROWS, QL), BF16),
        vm((2, MINE, 2 * ROWS, QL), BF16),
        vm((2, MINE, 2, ROWS, QL), BF16),
        vm((2, MINE, ROWS, QL), BF16),
        vm((MINE, ROWS, QL), BF16),
        vm((MINE, ROWS, QL), BF16),
        vm((nz, MINE, ROWS, QL), BF16),
        vm((MINE, ROWS, QL), BF16),
        vm((MINE, ROWS, QL), BF16),
        vm((2, MINE, ROWS, QL), BF16),
        vm((2, MINE, 2, ROWS, QL), BF16),
        vm((2, MINE, 2 * ROWS, QL), BF16),
        vm((2, MINE, 2, 2 * ROWS, QL), BF16),
        vm((2, MINE, N, QL), BF16),
        vm((2, MINE, N, QL), BF16),
        vm((2, MINE, N, QL), BF16),
        vm((4, ROWS, QL), F32),
        vm((QUARTERS, 1, QL), F32),
        vm((8, 128), F32),
        vm((2 * NY, 8, 128), F32),
        vm((8, 128), F32),
        vm((nz, 8, 128), F32),
        dma((CHUNKS,)), dma((CHUNKS,)),
        dma((7 + 2 * NY,)), dma((8,)),
        dma((7,)), dma((7,)),
        dma((nz - 1,)), dma((nz - 1,)),
        dma((nz,)), dma((nz,)),
        dma((CHUNKS, nz)), dma((CHUNKS, nz)),
        dma((CHUNKS, nz // 2)), dma((CHUNKS,)),
        dma((2, CHUNKS)), dma((2, CHUNKS)),
        dma((2, CHUNKS)), dma((2, CHUNKS)),
        dma((2, CHUNKS)), dma((2, CHUNKS)),
        dma((MINE // 4,)), dma((MINE // 4,)),
        dma((2, CHUNKS)), dma((2, CHUNKS)),
        dma((2, CHUNKS)), dma((2, CHUNKS)),
        dma((2, CHUNKS)), dma((2, CHUNKS)),
    ]
    return pl.pallas_call(
        make_kernel(nx, nz),
        out_shape=(
            jax.ShapeDtypeStruct((T, H * D), BF16),
            jax.ShapeDtypeStruct((T, GROUPS * N), BF16),
            jax.ShapeDtypeStruct((T, GROUPS * N), BF16),
            jax.ShapeDtypeStruct((1, H), F32),
        ),
        in_specs=[pl.BlockSpec(memory_space=pltpu.VMEM)] * 9,
        out_specs=[pl.BlockSpec(memory_space=pltpu.VMEM)] * 4,
        scratch_shapes=scratch,
        compiler_params=pltpu.CompilerParams(vmem_limit_bytes=62 * 2**20, collective_id=0, has_side_effects=True),
        name="mixer_backward",
    )


def on_device(previous, saved_head_inputs, input_b, input_c, steps, decay_rate, skip_gain, segment_ids, advantage_mask):
    kernel = call(lax.axis_size("pipe"), lax.axis_size("seq_0"))
    gx, gb, gc, sk = kernel(
        previous[0],
        saved_head_inputs[0],
        input_b[0],
        input_c[0],
        steps[0],
        decay_rate,
        skip_gain,
        segment_ids,
        advantage_mask[None],
    )
    return gx[None], gb[None], gc[None], sk


def solution(mesh):
    finer = Mesh(
        mesh.devices.reshape(mesh.shape["pipe"], mesh.shape["seq"] // (2 * NY), NY, 2),
        ("pipe", "seq_0", "seq_1", "seq_2"),
    )
    return jax.shard_map(
        on_device,
        mesh=finer,
        in_specs=(
            P("pipe", SEQ, None),
            P("pipe", SEQ, None),
            P("pipe", SEQ, None),
            P("pipe", SEQ, None),
            P("pipe", SEQ, None),
            P("pipe", None),
            P("pipe", None),
            P("pipe", SEQ),
            P(SEQ),
        ),
        out_specs=(
            P("pipe", SEQ, None),
            P("pipe", SEQ, None),
            P("pipe", SEQ, None),
            P("pipe", None),
        ),
        check_vma=False,
    )
```

time: 123 us -> 98.7 us (0.80)
  Pallas kernels: 116 us -> 92.9 us
    pallas_call x1, Pallas kernels: 116 us -> 92.9 us  [on_device(): kernel(previous[0], saved_head_inputs[0], input_b[0], input_c[0], steps[0...]
    reshape x1 -> x0, local copies, waits for them, and re-layouts: 1.33 us -> none  [on_device(): return (gx[None], gb[None], gc[None], sk[:, :4].reshape(1, H))]
    unnamed x7 -> x10, local copies, waits for them, and re-layouts: 4.56 us -> 5.08 us
where the time goes in v2:
time: 98.7 us; the launch traced here: 98.6 us
  Pallas kernels  92.9 us (94%)
  local copies, waits for them, and re-layouts  5.08 us (5%)
    pallas_call x1, Pallas kernels, on_device(): kernel(previous[0], saved_head_inputs[0], input_b[0], input_c[0], steps[0...  92.9 us
    unnamed x10, local copies, waits for them, and re-layouts  5.08 us

profile of v2, /device:TPU:1, one launch (start us, length us, event | category | flops | bytes accessed | tf_op | source)
XLA Modules:
  0.0 98.6 jit_solution(4173027233233912226)
XLA Ops:
  0.6 92.9 %mixer_backward.1 = (bf16[128,8192]{1,0:T(8,128)(2,1)}, bf16[128,1024]{1,0:T(8,128)(2,1)}, bf16[128,1024]{1,0:T(8,128)(2,1)}, f32[1,128]{1,0:T(1,128)}) custom-call(bf16[128,8192]{1,0:T(8,128)(2,1)} %bitcast.9, bf16[128,8192]{1,0:T(8,128)(2,1)} %bitcast.10, bf16[128,1024]{1,0:T(8,128)(2,1)} %bitcast.12, bf16[128,1024]{1,0:T(8,128)(2,1)} %bitcast.13, ...), custom_call_target="tpu_custom_call" | custom-call | tf_op jit(solution)/shard_map/mixer_backward/pallas_call | solution.py:774
  93.5 0.0 copy-start.1
  93.5 0.0 copy-start
  93.5 0.0 copy-start.2
  93.5 3.1 %copy.17 = bf16[1,128,8192]{2,1,0:T(8,128)(2,1)} copy(bf16[1,128,8192]{2,1,0:T(8,128)(2,1)} %bitcast.11) | data formatting | bytes 4194304
  96.7 0.0 copy-done.1
  96.7 0.7 copy.18
  97.4 0.0 copy-done
  97.4 0.7 copy.19
  98.1 0.0 copy-done.2
  98.1 0.5 copy.20
Async XLA Ops:
  93.5 3.2 %copy-start.1 = (bf16[128,1024]{1,0:T(8,128)(2,1)S(1)}, bf16[128,1024]{1,0:T(8,128)(2,1)}, u32[]{:S(2)}) copy-start(bf16[128,1024]{1,0:T(8,128)(2,1)} %get-tuple-element.9) | copy-start | bytes 786436
  93.5 3.9 %copy-start = (bf16[128,1024]{1,0:T(8,128)(2,1)S(1)}, bf16[128,1024]{1,0:T(8,128)(2,1)}, u32[]{:S(2)}) copy-start(bf16[128,1024]{1,0:T(8,128)(2,1)} %get-tuple-element.10) | copy-start | bytes 786436
  93.5 4.6 %copy-start.2 = (f32[1,128]{1,0:T(1,128)S(1)}, f32[1,128]{1,0:T(1,128)}, u32[]{:S(2)}) copy-start(f32[1,128]{1,0:T(1,128)} %get-tuple-element.19) | copy-start | bytes 1540

commit v3 on v2

--- a/solution.py
+++ b/solution.py
@@ -56,8 +56,9 @@
     count = (MINE // 4, CHUNKS)
 
     def kernel(
-        prev_ref, x_ref, b_ref, c_ref, steps_ref, rate_ref, skip_ref, seg_ref, mask_ref,
+        prev_ref, x_hbm, b_hbm, c_hbm, steps_hbm, rate_ref, skip_ref, seg_ref, mask_ref,
         gx_out, gb_out, gc_out, sk_out,
+        x_ref, b_ref, c_ref, steps_ref, lsem,
         grad, xo, gi, gxa, lexp, gca, gba, cum_s, cumt_s, bias_s, biast_s, eexp, lvs, bt, ct, wide_s, fz_s, fz_r, fzx,
         info_s, info_r, th_s, thx,
         st, sp, tt, t1, us, u2, zs, zr, az, ho, hi, vo, vi, eo, er, keep, epart, ex, tz_s,
@@ -84,6 +85,19 @@
         def z_peer(off):
             return (px, lax.rem(z + off, nz), y, c)
 
+        loads = [
+            pltpu.make_async_copy(src, dst, lsem.at[i])
+            for i, (src, dst) in enumerate(
+                ((steps_hbm, steps_ref), (b_hbm, b_ref), (c_hbm, c_ref), (x_hbm, x_ref), (prev_ref, grad))
+            )
+        ]
+        for load in loads[:4]:
+            load.start()
+
+        @pl.when(px == nx - 1)
+        def _():
+            loads[4].start()
+
         barrier = pltpu.get_barrier_semaphore()
 
         def greet(where):
@@ -122,6 +136,7 @@
 
         row = lax.broadcasted_iota(jnp.int32, (T, T), 0)
         col = lax.broadcasted_iota(jnp.int32, (T, T), 1)
+        loads[0].wait()
         cum = -(steps_ref[...] * rate_ref[...])
         for shift in (1, 2, 4, 8, 16, 32, 64):
             cum = cum + jnp.where(row >= shift, pltpu.roll(cum, shift, 0), 0.0)
@@ -163,6 +178,13 @@
         lvs[...] = jnp.concatenate(split(leave, 2), axis=1)
         kept = jnp.broadcast_to(mask_ref[...].astype(F32), (T, T)).T
         wide_s[...] = jnp.concatenate([kept, kept], axis=1)
+
+        for load in loads[1:4]:
+            load.wait()
+
+        @pl.when(px == nx - 1)
+        def _():
+            loads[4].wait()
 
         for g in range(GROUPS):
             part = slice(N * g, N * g + N)
@@ -579,7 +601,7 @@
                 def _():
                     for i in range(4):
                         part = lanes_of(4 * k + i, QL)
-                        grad[:, part] = (prev_ref[:, part].astype(F32) * wide_s[...]).astype(BF16)
+                        grad[:, part] = (grad[:, part].astype(F32) * wide_s[...]).astype(BF16)
 
                 @pl.when(px < nx - 1)
                 def _():
@@ -606,25 +628,41 @@
             def _():
                 sk_plane()
 
-            at(1, count[1], lambda i: pair_step(1, i))
-            at(2, count[1], plane_send)
-            at(back_at, count[1], plane_back)
-            at(back_at + 1, count[1], lambda i: pair_out(1, i))
-            at(back_at + 2, count[1], lambda i: hand_back(1, i))
+            def at_pairing_end(lag, n, step):
+                @pl.when((k >= lag) & (k < lag + n - 1))
+                def _():
+                    step(k - lag)
+
+                @pl.when(k == lag + n - 2)
+                def _():
+                    step(k - lag + 1)
+
+            def two(step):
+                def both(i):
+                    step(2 * i)
+                    step(2 * i + 1)
+
+                return both
+
+            at_pairing_end(1, count[1], lambda i: pair_step(1, i))
+            at_pairing_end(2, count[1], plane_send)
+            at_pairing_end(back_at, count[1], plane_back)
+            at_pairing_end(back_at + 1, count[1], lambda i: pair_out(1, i))
+            at_pairing_end(back_at + 2, count[1], lambda i: hand_back(1, i))
 
             @pl.when(k == CHUNKS + 2)
             def _():
                 sk_along()
 
-            at(back_at + 3, count[1], finish_b)
-            at(1, count[0], lambda i: pair_step(0, i))
-            at(chain_at, count[0], chain)
+            at_pairing_end(back_at + 3, count[1], finish_b)
+            at(1, count[0] // 2, two(lambda i: pair_step(0, i)))
+            at(chain_at, count[0] // 2, two(chain))
             at(chain_at + 1, count[0], lambda i: pair_out(0, i))
             at(chain_at + 2, count[0], lambda i: hand_back(0, i))
             at(chain_at + 3, count[0], finish_c)
             return carry
 
-        lax.fori_loop(0, CHUNKS + 7, main, 0)
+        lax.fori_loop(0, CHUNKS + 6, main, 0)
 
         for off in range(1, nz):
             skz_copy(off).wait_recv()
@@ -691,6 +729,11 @@
     vm = pltpu.VMEM
     dma = pltpu.SemaphoreType.DMA
     scratch = [
+        vm((T, H * D), BF16),
+        vm((T, GROUPS * N), BF16),
+        vm((T, GROUPS * N), BF16),
+        vm((T, H), F32),
+        dma((5,)),
         vm((T, H * D), BF16),
         vm((QUARTERS, T, QL), BF16),
         vm((QUARTERS, T, QL), BF16),
@@ -756,17 +799,38 @@
     return pl.pallas_call(
         make_kernel(nx, nz),
         out_shape=(
-            jax.ShapeDtypeStruct((T, H * D), BF16),
-            jax.ShapeDtypeStruct((T, GROUPS * N), BF16),
-            jax.ShapeDtypeStruct((T, GROUPS * N), BF16),
-            jax.ShapeDtypeStruct((1, H), F32),
+            vm((T, H * D), BF16),
+            vm((T, GROUPS * N), BF16),
+            vm((T, GROUPS * N), BF16),
+            vm((1, H), F32),
         ),
-        in_specs=[pl.BlockSpec(memory_space=pltpu.VMEM)] * 9,
+        in_specs=[pl.BlockSpec(memory_space=pl.ANY)] * 5 + [pl.BlockSpec(memory_space=pltpu.VMEM)] * 4,
         out_specs=[pl.BlockSpec(memory_space=pltpu.VMEM)] * 4,
         scratch_shapes=scratch,
-        compiler_params=pltpu.CompilerParams(vmem_limit_bytes=62 * 2**20, collective_id=0, has_side_effects=True),
+        compiler_params=pltpu.CompilerParams(vmem_limit_bytes=56 * 2**20, collective_id=0, has_side_effects=True),
         name="mixer_backward",
     )
+
+
+def deliver(*results):
+    def kernel(*refs):
+        n = len(results)
+        sem = refs[2 * n]
+        copies = [pltpu.make_async_copy(refs[i], refs[n + i], sem.at[i]) for i in range(n)]
+        for copy in copies:
+            copy.start()
+        for copy in copies:
+            copy.wait()
+
+    return pl.pallas_call(
+        kernel,
+        out_shape=tuple(jax.ShapeDtypeStruct(v.shape, v.dtype) for v in results),
+        in_specs=[pl.BlockSpec(memory_space=pltpu.VMEM)] * len(results),
+        out_specs=[pl.BlockSpec(memory_space=pl.ANY)] * len(results),
+        scratch_shapes=[pltpu.SemaphoreType.DMA((len(results),))],
+        compiler_params=pltpu.CompilerParams(vmem_limit_bytes=2**20),
+        name="deliver",
+    )(*results)
 
 
 def on_device(previous, saved_head_inputs, input_b, input_c, steps, decay_rate, skip_gain, segment_ids, advantage_mask):
@@ -782,6 +846,7 @@
         segment_ids,
         advantage_mask[None],
     )
+    gx, gb, gc, sk = deliver(gx, gb, gc, sk)
     return gx[None], gb[None], gc[None], sk
 
 

time: 98.7 us -> 92.7 us (0.939)
  local copies, waits for them, and re-layouts: 5.08 us -> 0 us
    unnamed x10 -> x0, local copies, waits for them, and re-layouts: 5.08 us -> none
    pallas_call x1, Pallas kernels: 92.9 us -> 90.5 us  [on_device(): kernel(previous[0], saved_head_inputs[0], input_b[0], input_c[0], steps[0...]
    pallas_call x0 -> x1, Pallas kernels: none -> 1.52 us  [deliver(): pl.pallas_call(kernel, out_shape=tuple((jax.ShapeDtypeStruct(v.shape, v.d...]
where the time goes in v3:
time: 92.7 us; the launch traced here: 92.6 us
  Pallas kernels  92 us (99%)
    pallas_call x1, Pallas kernels, on_device(): kernel(previous[0], saved_head_inputs[0], input_b[0], input_c[0], steps[0...  90.5 us

profile of v3, /device:TPU:1, one launch (start us, length us, event | category | flops | bytes accessed | tf_op | source)
XLA Modules:
  0.0 92.6 jit_solution(7222610211914421897)
XLA Ops:
  0.6 90.5 %mixer_backward.1 = (bf16[128,8192]{1,0:T(8,128)(2,1)S(1)}, bf16[128,1024]{1,0:T(8,128)(2,1)S(1)}, bf16[128,1024]{1,0:T(8,128)(2,1)S(1)}, f32[1,128]{1,0:T(1,128)S(1)}) custom-call(bf16[128,8192]{1,0:T(8,128)(2,1)} %bitcast.9, bf16[128,8192]{1,0:T(8,128)(2,1)} %bitcast.10, bf16[128,1024]{1,0:T(8,128)(2,1)} %bitcast.11, bf16[128,1024]{1,0:T(8,128)(2,1)} %bitcast.12, ...), custom_call_target="tpu_custom_call" | custom-call | tf_op jit(solution)/shard_map/mixer_backward/pallas_call | solution.py:838
  91.1 1.5 %deliver.1 = (bf16[128,8192]{1,0:T(8,128)(2,1)}, bf16[128,1024]{1,0:T(8,128)(2,1)}, bf16[128,1024]{1,0:T(8,128)(2,1)}, f32[1,128]{1,0:T(1,128)}) custom-call(bf16[128,8192]{1,0:T(8,128)(2,1)S(1)} %get-tuple-element.12.refs_0_, bf16[128,1024]{1,0:T(8,128)(2,1)S(1)} %get-tuple-element.13.refs_1_, bf16[128,1024]{1,0:T(8,128)(2,1)S(1)} %get-tuple-element.14.refs_2_, ...), custom_call_target="tpu_custom_call" | custom-call | tf_op jit(solution)/shard_map/deliver/pallas_call | solution.py:825

commit v4 on v3

--- a/solution.py
+++ b/solution.py
@@ -72,6 +72,9 @@
         c = lax.axis_index("seq_2")
         d = 2 * y + c
         last_d = 2 * NY - 1
+        half = nz // 2
+        start = half * lax.div(z, half)
+        to_top = (z >= half) & (z < nz - 1)
 
         def remote(src, dst, ssem, rsem, where):
             return pltpu.make_async_remote_copy(
@@ -293,12 +296,13 @@
             m = pl.ds(width[1] * k, width[1])
             return remote(az.at[z, m], az.at[z, m], asend.at[k, other], arecv.at[k, z], (px, other, y, c))
 
-        half = nz // 2
-        start = half * lax.div(z, half)
-
         def down(k, other):
             m = pl.ds(width[1] * k, width[1])
             return remote(ho.at[m], hi.at[m], hsend.at[k, other], hrecv.at[k], (px, other, y, c))
+
+
+        nearer = tuple(range(half // 2, half))
+        farther = tuple(range(half // 2))
 
         def arrived(k, source):
             m = pl.ds(width[1] * k, width[1])
@@ -366,6 +370,16 @@
 
             lax.fori_loop(start, z, body, 0)
 
+            @pl.when(to_top)
+            def _():
+                across(k, nz - 1).start()
+
+        def hand_down(k, others):
+            for i in range(width[1]):
+                ho[width[1] * k + i] = tz_s[2 + i].astype(BF16)
+            for other in others:
+                down(k, other).start()
+
         def plane_back(k):
             @pl.when(z >= half)
             def _():
@@ -394,9 +408,21 @@
                 for i in range(width[1]):
                     m = width[1] * k + i
                     total, factor = plane_total(1, m)
-                    ho[m] = (factor * tz_s[i] + total).astype(BF16)
-                for other in range(half):
-                    down(k, other).start()
+                    tz_s[2 + i] = factor * tz_s[i] + total
+                hand_down(k, nearer)
+
+            @pl.when(z == nz - 1)
+            def _():
+                for i in range(width[1]):
+                    tz_s[2 + i] = plane_total(1, width[1] * k + i)[0]
+                for t in range(half - 1):
+                    source = nz - 2 - t
+                    arrived(k, source).wait_recv()
+                    for i in range(width[1]):
+                        m = width[1] * k + i
+                        factor = fzx[quarter(m, mine), source : source + 1, :]
+                        tz_s[2 + i] = factor * tz_s[2 + i] + az[source, m].astype(F32)
+                hand_down(k, farther)
 
             spread_out(1, k, [tz_s[i] for i in range(width[1])])
 
@@ -480,6 +506,10 @@
             return carry
 
         lax.fori_loop(0, z, f_start, 0)
+        @pl.when(to_top)
+        def _():
+            f_copy(nz - 1).start()
+
 
         def table(k, carry):
             rows = jnp.concatenate(split(th_s[...], 3), axis=1)
@@ -508,8 +538,18 @@
 
         def plane_table():
             lax.fori_loop(0, nz - 1 - z, f_wait, 0)
+
+            @pl.when(z == nz - 1)
+            def _():
+                for source in range(half, nz - 1):
+                    f_arrived(source).wait_recv()
+
             everything = jnp.concatenate(
-                [jnp.where(i > z, fz_r[i, 0:1, :], 0.0) for i in range(nz)], axis=0
+                [
+                    jnp.where((i > z) | (z == nz - 1 if half <= i < nz - 1 else False), fz_r[i, 0:1, :], 0.0)
+                    for i in range(nz)
+                ],
+                axis=0,
             )
             th_s[0:nz, :] = everything
 
@@ -624,10 +664,6 @@
             def _():
                 plane_table()
 
-            @pl.when(k == CHUNKS)
-            def _():
-                sk_plane()
-
             def at_pairing_end(lag, n, step):
                 @pl.when((k >= lag) & (k < lag + n - 1))
                 def _():
@@ -644,9 +680,21 @@
 
                 return both
 
-            at_pairing_end(1, count[1], lambda i: pair_step(1, i))
-            at_pairing_end(2, count[1], plane_send)
+            at(1, count[1] - 1, lambda i: pair_step(1, i))
+            at(2, count[1] - 2, plane_send)
+
+            @pl.when(k == CHUNKS)
+            def _():
+                plane_send(CHUNKS - 1)
+                sk_plane()
+
             at_pairing_end(back_at, count[1], plane_back)
+
+            @pl.when(k == CHUNKS - 1)
+            def _():
+                pair_step(1, k)
+                plane_send(k - 1)
+
             at_pairing_end(back_at + 1, count[1], lambda i: pair_out(1, i))
             at_pairing_end(back_at + 2, count[1], lambda i: hand_back(1, i))
 
@@ -656,9 +704,25 @@
 
             at_pairing_end(back_at + 3, count[1], finish_b)
             at(1, count[0] // 2, two(lambda i: pair_step(0, i)))
+
+            @pl.when(z < nz - 1)
+            def _():
+                at(chain_at + 1, count[0], lambda i: pair_out(0, i))
+
+            @pl.when(z == nz - 1)
+            def _():
+                at(chain_at + 1, count[0] // 2, two(lambda i: pair_out(0, i)))
+
             at(chain_at, count[0] // 2, two(chain))
-            at(chain_at + 1, count[0], lambda i: pair_out(0, i))
-            at(chain_at + 2, count[0], lambda i: hand_back(0, i))
+
+            @pl.when(z < nz - 1)
+            def _():
+                at(chain_at + 2, count[0], lambda i: hand_back(0, i))
+
+            @pl.when(z == nz - 1)
+            def _():
+                at(chain_at + 2, count[0] // 2, two(lambda i: hand_back(0, i)))
+
             at(chain_at + 3, count[0], finish_c)
             return carry
 
@@ -713,14 +777,28 @@
 
                     lax.fori_loop(start, z, let_go, 0)
 
+                    @pl.when(to_top)
+                    def _(k=k):
+                        across(k, nz - 1).wait_send()
+
                     @pl.when(z == half)
-                    def _():
-                        for other in range(half):
+                    def _(k=k):
+                        for other in nearer:
+                            down(k, other).wait_send()
+
+                    @pl.when(z == nz - 1)
+                    def _(k=k):
+                        for other in farther:
                             down(k, other).wait_send()
 
 
             each(count[w], drain)
         each(z, lambda other: f_copy(other).wait_send())
+
+        @pl.when(to_top)
+        def _():
+            f_copy(nz - 1).wait_send()
+
 
     return kernel
 
@@ -787,7 +865,7 @@
         dma((nz - 1,)), dma((nz - 1,)),
         dma((nz,)), dma((nz,)),
         dma((CHUNKS, nz)), dma((CHUNKS, nz)),
-        dma((CHUNKS, nz // 2)), dma((CHUNKS,)),
+        dma((CHUNKS, nz)), dma((CHUNKS,)),
         dma((2, CHUNKS)), dma((2, CHUNKS)),
         dma((2, CHUNKS)), dma((2, CHUNKS)),
         dma((2, CHUNKS)), dma((2, CHUNKS)),

time: 92.7 us -> 92.4 us (level)
  no operation moved by 1% of the time
where the time goes in v4:
time: 92.4 us; the launch traced here: 92 us
  Pallas kernels  91.3 us (99%)
    pallas_call x1, Pallas kernels, on_device(): kernel(previous[0], saved_head_inputs[0], input_b[0], input_c[0], steps[0...  89.8 us

profile of v4, /device:TPU:1, one launch (start us, length us, event | category | flops | bytes accessed | tf_op | source)
XLA Modules:
  0.0 92.0 jit_solution(14342286818179811215)
XLA Ops:
  0.6 89.8 %mixer_backward.1 = (bf16[128,8192]{1,0:T(8,128)(2,1)S(1)}, bf16[128,1024]{1,0:T(8,128)(2,1)S(1)}, bf16[128,1024]{1,0:T(8,128)(2,1)S(1)}, f32[1,128]{1,0:T(1,128)S(1)}) custom-call(bf16[128,8192]{1,0:T(8,128)(2,1)} %bitcast.9, bf16[128,8192]{1,0:T(8,128)(2,1)} %bitcast.10, bf16[128,1024]{1,0:T(8,128)(2,1)} %bitcast.11, bf16[128,1024]{1,0:T(8,128)(2,1)} %bitcast.12, ...), custom_call_target="tpu_custom_call" | custom-call | tf_op jit(solution)/shard_map/mixer_backward/pallas_call | solution.py:916
  90.5 1.5 %deliver.1 = (bf16[128,8192]{1,0:T(8,128)(2,1)}, bf16[128,1024]{1,0:T(8,128)(2,1)}, bf16[128,1024]{1,0:T(8,128)(2,1)}, f32[1,128]{1,0:T(1,128)}) custom-call(bf16[128,8192]{1,0:T(8,128)(2,1)S(1)} %get-tuple-element.12.refs_0_, bf16[128,1024]{1,0:T(8,128)(2,1)S(1)} %get-tuple-element.13.refs_1_, bf16[128,1024]{1,0:T(8,128)(2,1)S(1)} %get-tuple-element.14.refs_2_, ...), custom_call_target="tpu_custom_call" | custom-call | tf_op jit(solution)/shard_map/deliver/pallas_call | solution.py:903

commit v5 on v4

--- a/solution.py
+++ b/solution.py
@@ -59,7 +59,7 @@
         prev_ref, x_hbm, b_hbm, c_hbm, steps_hbm, rate_ref, skip_ref, seg_ref, mask_ref,
         gx_out, gb_out, gc_out, sk_out,
         x_ref, b_ref, c_ref, steps_ref, lsem,
-        grad, xo, gi, gxa, lexp, gca, gba, cum_s, cumt_s, bias_s, biast_s, eexp, lvs, bt, ct, wide_s, fz_s, fz_r, fzx,
+        grad, xo, gi, gxa, lexp, gca, gba, cum_s, cumt_s, bias_s, biast_s, eexp, lvs, ens, bt, ct, wide_s, fz_s, fz_r, fzx,
         info_s, info_r, th_s, thx,
         st, sp, tt, t1, us, u2, zs, zr, az, ho, hi, vo, vi, eo, er, keep, epart, ex, tz_s,
         skp, sk_s, sk_r, skz_s, skz_r,
@@ -471,7 +471,7 @@
             states(0, k, mine)
             return carry
 
-        lax.fori_loop(0, count[0], fwd_states, 0)
+        lax.fori_loop(0, count[0] // 2, fwd_states, 0)
 
         for off in range(1, 2 * NY):
             info_copy(off).wait_recv()
@@ -488,7 +488,6 @@
         enter_from = info_r[lax.rem(d + 2 * NY, 2 * NY + 1), 1:2, :]
         segc = jnp.broadcast_to(seg_ref[...].astype(F32), (T, T)).T
         enter = jnp.exp(cum_s[...]) * jnp.where(segc == enter_from, 1.0, 0.0)
-        lvs[...] = jnp.concatenate(split(enter, 2), axis=1)
         whole = th_s[0:1, :]
         for i in range(1, 2 * NY):
             whole = whole * th_s[i : i + 1, :]
@@ -518,19 +517,22 @@
             return carry
 
         lax.fori_loop(0, QUARTERS // 4, table, 0)
+        ens[...] = jnp.concatenate(split(enter, 2), axis=1)
 
         def fwd_chip(k, carry):
             chip_state(0, k)
             return carry
 
-        lax.fori_loop(0, count[0], fwd_chip, 0)
+        lax.fori_loop(0, count[0] // 2, fwd_chip, 0)
 
         def enter_wide(k, carry):
             for i in range(4):
-                eexp[4 * k + i] = dot(lvs[...], indicator(4 * k + i, 2))
+                eexp[4 * k + i] = dot(ens[...], indicator(4 * k + i, 2))
             return carry
 
         enter_wide(0, 0)
+        lax.fori_loop(count[0] // 2, count[0], fwd_states, 0)
+        lax.fori_loop(count[0] // 2, count[0], fwd_chip, 0)
 
         def f_wait(t, carry):
             f_arrived(nz - 1 - t).wait_recv()
@@ -627,6 +629,49 @@
 
             lax.fori_loop(0, n, body, 0)
 
+        def settle():
+            @pl.when(px > 0)
+            def _():
+                each(CHUNKS, lambda k: grad_copy(k).wait_send())
+
+            for off in range(1, 2 * NY):
+                info_copy(off).wait_send()
+
+            @pl.when((d == last_d) & (z < nz - 1))
+            def _():
+                for other in range(2 * NY):
+                    info_next(other).wait_send()
+
+            for w in range(2):
+
+                def drain(k, w=w):
+                    partner_copy(w, k).wait_send()
+                    t_copy(w, k).wait_send()
+                    u_copy(w, k).wait_send()
+                    if w == 0:
+
+                        @pl.when(z < nz - 1)
+                        def _():
+                            chain_copy(k).wait_send()
+                    else:
+
+                        def let_go(other, carry, k=k):
+                            across(k, other).wait_send()
+                            return carry
+
+                        lax.fori_loop(start, z, let_go, 0)
+
+                        @pl.when(to_top)
+                        def _(k=k):
+                            across(k, nz - 1).wait_send()
+
+                each(count[w], drain)
+            each(z, lambda other: f_copy(other).wait_send())
+
+            @pl.when(to_top)
+            def _():
+                f_copy(nz - 1).wait_send()
+
         chain_at = 2 + lax.div(z * 5 + 3, nz - 1)
         back_at = jnp.where(z < half, 4, 3)
 
@@ -702,6 +747,10 @@
             def _():
                 sk_along()
 
+            @pl.when(k == CHUNKS + 3)
+            def _():
+                settle()
+
             at_pairing_end(back_at + 3, count[1], finish_b)
             at(1, count[0] // 2, two(lambda i: pair_step(0, i)))
 
@@ -735,51 +784,18 @@
             acc = acc + skz_r[i]
         sk_out[...] = acc[0:1, :]
 
-        @pl.when(px > 0)
-        def _():
-            def body(k, carry):
-                grad_copy(k).wait_send()
-                return carry
-
-            lax.fori_loop(0, CHUNKS, body, 0)
-
         for off in range(1, 2 * NY):
-            info_copy(off).wait_send()
             sk_copy(off).wait_send()
-
-        @pl.when((d == last_d) & (z < nz - 1))
-        def _():
-            for other in range(2 * NY):
-                info_next(other).wait_send()
-
         for off in range(1, nz):
             skz_copy(off).wait_send()
 
         for w in range(2):
 
             def drain(k, w=w):
-                partner_copy(w, k).wait_send()
                 back_copy(w, k).wait_send()
-                t_copy(w, k).wait_send()
-                u_copy(w, k).wait_send()
                 v_copy(w, k).wait_send()
                 e_copy(w, k).wait_send()
-                if w == 0:
-
-                    @pl.when(z < nz - 1)
-                    def _():
-                        chain_copy(k).wait_send()
-                else:
-
-                    def let_go(other, carry, k=k):
-                        across(k, other).wait_send()
-                        return carry
-
-                    lax.fori_loop(start, z, let_go, 0)
-
-                    @pl.when(to_top)
-                    def _(k=k):
-                        across(k, nz - 1).wait_send()
+                if w == 1:
 
                     @pl.when(z == half)
                     def _(k=k):
@@ -791,14 +807,7 @@
                         for other in farther:
                             down(k, other).wait_send()
 
-
             each(count[w], drain)
-        each(z, lambda other: f_copy(other).wait_send())
-
-        @pl.when(to_top)
-        def _():
-            f_copy(nz - 1).wait_send()
-
 
     return kernel
 
@@ -824,6 +833,7 @@
         vm((T, T), F32),
         vm((T, T), F32),
         vm((QUARTERS, T, QL), F32),
+        vm((T, 2 * H), BF16),
         vm((T, 2 * H), BF16),
         vm((GROUPS, N, T), BF16),
         vm((GROUPS, N, T), BF16),

time: 92.4 us -> 92.3 us (level)
  no operation moved by 1% of the time
where the time goes in v5:
time: 92.3 us; the launch traced here: 91.8 us
  Pallas kernels  91.2 us (99%)
    pallas_call x1, Pallas kernels, on_device(): kernel(previous[0], saved_head_inputs[0], input_b[0], input_c[0], steps[0...  89.7 us

profile of v5, /device:TPU:1, one launch (start us, length us, event | category | flops | bytes accessed | tf_op | source)
XLA Modules:
  0.0 91.8 jit_solution(9866611891187941447)
XLA Ops:
  0.6 89.7 %mixer_backward.1 = (bf16[128,8192]{1,0:T(8,128)(2,1)S(1)}, bf16[128,1024]{1,0:T(8,128)(2,1)S(1)}, bf16[128,1024]{1,0:T(8,128)(2,1)S(1)}, f32[1,128]{1,0:T(1,128)S(1)}) custom-call(bf16[128,8192]{1,0:T(8,128)(2,1)} %bitcast.9, bf16[128,8192]{1,0:T(8,128)(2,1)} %bitcast.10, bf16[128,1024]{1,0:T(8,128)(2,1)} %bitcast.11, bf16[128,1024]{1,0:T(8,128)(2,1)} %bitcast.12, ...), custom_call_target="tpu_custom_call" | custom-call | tf_op jit(solution)/shard_map/mixer_backward/pallas_call | solution.py:926
  90.3 1.5 %deliver.1 = (bf16[128,8192]{1,0:T(8,128)(2,1)}, bf16[128,1024]{1,0:T(8,128)(2,1)}, bf16[128,1024]{1,0:T(8,128)(2,1)}, f32[1,128]{1,0:T(1,128)}) custom-call(bf16[128,8192]{1,0:T(8,128)(2,1)S(1)} %get-tuple-element.12.refs_0_, bf16[128,1024]{1,0:T(8,128)(2,1)S(1)} %get-tuple-element.13.refs_1_, bf16[128,1024]{1,0:T(8,128)(2,1)S(1)} %get-tuple-element.14.refs_2_, ...), custom_call_target="tpu_custom_call" | custom-call | tf_op jit(solution)/shard_map/deliver/pallas_call | solution.py:913
